TPU v7x, 128 devices: a whole 4x4x4 slice. The times are simulated.
128 devices in a mesh: rep: 4 (over y_lo, core), site: 32 (over z, x, y_hi).
Axes of the slice: x: 4, y: 4 (y_hi: 2, y_lo: 2; y = y_hi * 2 + y_lo), z: 4, core: 2. Of those that a mesh axis runs over, the one named last changes fastest.
Arguments:
- working: bfloat16 [4, 32, 16, 64, 2304], P('rep', 'site'), may hold values from -4 to 4
- master_slots: float32 [32, 4, 4, 64, 2304], P('site', 'rep'), may hold values from -4 to 4
- accum_slots: float32 [32, 4, 4, 64, 2304], P('site', 'rep'), may hold values from 0.01 to 1
- pool_images: bfloat16 [4, 256, 32, 1024], P(None, None, 'site'), may hold values from -6 to 6
- pool_targets: bfloat16 [4, 32, 16, 64, 256], P(None, 'site'), may hold values from -0.8984375 to 0.8984375
- batch_index: int32 [4, 3], replicated, may hold values from 0 to 3
- owner_map: int32 [4], replicated, may hold values from 0 to 3, each once
Outputs:
- working_next: bfloat16 [32, 16, 64, 2304], P('site')
- master_next: float32 [32, 4, 4, 64, 2304], P('site', 'rep')
- accum_next: float32 [32, 4, 4, 64, 2304], P('site', 'rep')
Inputs may be any that keep to these rules, and one draw needn't show every extreme that they name: `owner_map`: each replica owns exactly one shard.
All inputs are finite; a program needn't handle non-finite values.
Results may differ from a plain program's by a relative error of at most 0.015.
Values may be sent and summed in bfloat16 or wider, within the bound.
A program may use at most 192 MiB of HBM per device.

v0:
```python
import jax
import jax.numpy as jnp
from jax import lax
from jax.sharding import PartitionSpec as P

CHANNELS = 64
FIELD = 6
MICRO = 3


learning_rate = 0.3
epsilon = 1e-08


def passed_along(shard, axis, by):
    devices = lax.axis_size(axis)
    pairs = [(i, i + by) for i in range(devices) if 0 <= i + by < devices]
    return lax.ppermute(shard, axis, pairs)


def build_patches(window):
    batch_rows = window.shape[0]
    columns = window.shape[2] // CHANNELS
    grid_cells = window.reshape(batch_rows, FIELD, columns, CHANNELS)
    padded = jnp.pad(grid_cells, ((0, 0), (0, 0), (2, 3), (0, 0)))
    stacked = jnp.stack(
        [padded[:, :, offset : offset + columns, :] for offset in range(FIELD)], axis=2
    )
    return stacked.transpose(0, 3, 1, 2, 4).reshape(batch_rows, columns, FIELD * FIELD * CHANNELS)


def halo_rows(images):
    after_one = passed_along(images, "site", -1)
    paired = passed_along(jnp.concatenate([images, after_one], axis=1), "site", -2)
    after_two = paired[:, 0:1]
    after_three = paired[:, 1:2]
    before_one = passed_along(images, "site", 1)
    before_two = passed_along(before_one, "site", 1)
    return jnp.concatenate(
        [before_two, before_one, images, after_one, after_two, after_three], axis=1
    )


def per_device(
    working, master_slots, accum_slots, pool_images, pool_targets, batch_index, owner_map
):
    replica = lax.axis_index("rep")
    replicas = lax.axis_size("rep")
    chosen = lax.dynamic_index_in_dim(batch_index, replica, 0, keepdims=False)
    weights = working[0, 0]
    factor = weights.shape[2] ** (-0.5)
    gradient = jnp.zeros(weights.shape, jnp.float32)
    for micro_step in range(MICRO):
        images = lax.dynamic_index_in_dim(pool_images, chosen[micro_step], 0, keepdims=False)
        targets = lax.dynamic_index_in_dim(pool_targets, chosen[micro_step], 0, keepdims=False)[0]
        patches = build_patches(halo_rows(images))
        forward = factor * jnp.einsum(
            "bck,cok->cob", patches, weights, preferred_element_type=jnp.float32
        )
        active = jnp.tanh(forward)
        signal = ((active - targets.astype(jnp.float32)) * (1.0 - active * active)).astype(
            jnp.bfloat16
        )
        gradient = gradient + factor * jnp.einsum(
            "cob,bck->cok", signal, patches, preferred_element_type=jnp.float32
        )
    blocks = gradient.reshape(replicas, -1, weights.shape[1], weights.shape[2])
    ordered = jnp.take(blocks, owner_map, axis=0).astype(jnp.bfloat16)
    summed = lax.psum_scatter(ordered, "rep", scatter_dimension=0, tiled=True).astype(jnp.float32)[
        None
    ]
    accum_next = accum_slots + summed * summed
    master_next = master_slots - learning_rate * summed / (jnp.sqrt(accum_next) + epsilon)
    fetched = lax.all_gather(master_next[0].astype(jnp.bfloat16), "rep", axis=0, tiled=True)
    numbers = jnp.arange(replicas, dtype=jnp.int32)
    matches = (owner_map[:, None] == numbers[None, :]).astype(jnp.int32)
    inverse = jnp.sum(numbers[:, None] * matches, axis=0)
    working_next = jnp.take(fetched, inverse, axis=0).reshape(weights.shape)[None]
    return (working_next, master_next, accum_next)


def solution(mesh):
    placed = (
        P("rep", "site", None, None, None),
        P("site", "rep", None, None, None),
        P("site", "rep", None, None, None),
        P(None, None, "site", None),
        P(None, "site", None, None, None),
        P(),
        P(),
    )
    return jax.shard_map(
        per_device,
        mesh=mesh,
        in_specs=placed,
        out_specs=(
            P("site", None, None, None),
            P("site", "rep", None, None, None),
            P("site", "rep", None, None, None),
        ),
        check_vma=False,
    )
```

profile of v0, /device:TPU:17, one launch (start us, length us, event | category | flops | bytes accessed | tf_op | source)
XLA Modules:
  0.0 386.4 jit_solution(1213115903634701504)
XLA Ops:
  14.3 1.5 constant_dynamic-slice_fusion
  16.0 2.9 collective-permute-start
  18.9 4.7 %collective-permute-start.2 = (bf16[256,1,1024]{0,2,1:T(8,128)(2,1)S(1)}, bf16[256,1,1024]{0,2,1:T(8,128)(2,1)S(1)}, u32[]{:S(2)}, u32[]{:S(2)}) collective-permute-start(bf16[256,1,1024]{0,2,1:T(8,128)(2,1)S(1)} %bitcast.251), channel_id=1, source_target_pairs={{1,0},{2,1},{3,2},{4,3},{5,4},{6,5},{7,6},{8,7},{9,8},{10,9},{11,1... | collective-permute-start | bytes 1572872 | tf_op jit(solution)/shard_map/ppermute | solution.py:18
  23.8 3.0 collective-permute-start.4
  26.8 4.5 %collective-permute-start.6 = (bf16[256,1,1024]{0,2,1:T(8,128)(2,1)S(1)}, bf16[256,1,1024]{0,2,1:T(8,128)(2,1)S(1)}, u32[]{:S(2)}, u32[]{:S(2)}) collective-permute-start(bf16[256,1,1024]{0,2,1:T(8,128)(2,1)S(1)} %bitcast.246), channel_id=1, source_target_pairs={{1,0},{2,1},{3,2},{4,3},{5,4},{6,5},{7,6},{8,7},{9,8},{10,9},{11,1... | collective-permute-start | bytes 1572872 | tf_op jit(solution)/shard_map/ppermute | solution.py:18
  31.6 3.1 collective-permute-start.8
  34.7 19.9 %collective-permute-done = bf16[256,1,1024]{0,2,1:T(8,128)(2,1)} collective-permute-done((bf16[256,1,1024]{0,2,1:T(8,128)(2,1)S(1)}, bf16[256,1,1024]{0,2,1:T(8,128)(2,1)}, u32[]{:S(2)}, u32[]{:S(2)}) %collective-permute-start) | collective-permute-done | bytes 524320 | tf_op jit(solution)/shard_map/ppermute | solution.py:18
  54.7 1.9 collective-permute-start.10
  56.6 10.1 %collective-permute-done.2 = bf16[256,1,1024]{0,2,1:T(8,128)(2,1)S(1)} collective-permute-done((bf16[256,1,1024]{0,2,1:T(8,128)(2,1)S(1)}, bf16[256,1,1024]{0,2,1:T(8,128)(2,1)S(1)}, u32[]{:S(2)}, u32[]{:S(2)}) %collective-permute-start.2) | collective-permute-done | bytes 524320 | tf_op jit(solution)/shard_map/ppermute | solution.py:18
  66.8 4.0 %collective-permute-start.1 = (bf16[256,1,1024]{0,2,1:T(8,128)(2,1)}, bf16[256,1,1024]{0,2,1:T(8,128)(2,1)S(1)}, u32[]{:S(2)}, u32[]{:S(2)}) collective-permute-start(bf16[256,1,1024]{0,2,1:T(8,128)(2,1)} %collective-permute-done), channel_id=1, source_target_pairs={{0,1},{1,2},{2,3},{3,4},{4,5},{5,6},{6,7},{7,8},{8,9},{9,10},{10,1... | collective-permute-start | bytes 1572872 | tf_op jit(solution)/shard_map/ppermute | solution.py:18
  70.7 6.4 %collective-permute-done.4 = bf16[256,1,1024]{0,2,1:T(8,128)(2,1)} collective-permute-done((bf16[256,1,1024]{0,2,1:T(8,128)(2,1)S(1)}, bf16[256,1,1024]{0,2,1:T(8,128)(2,1)}, u32[]{:S(2)}, u32[]{:S(2)}) %collective-permute-start.4) | collective-permute-done | bytes 524320 | tf_op jit(solution)/shard_map/ppermute | solution.py:18
  77.2 2.0 collective-permute-start.5
  79.3 21.2 %collective-permute-done.6 = bf16[256,1,1024]{0,2,1:T(8,128)(2,1)S(1)} collective-permute-done((bf16[256,1,1024]{0,2,1:T(8,128)(2,1)S(1)}, bf16[256,1,1024]{0,2,1:T(8,128)(2,1)S(1)}, u32[]{:S(2)}, u32[]{:S(2)}) %collective-permute-start.6) | collective-permute-done | bytes 524320 | tf_op jit(solution)/shard_map/ppermute | solution.py:18
  101.8 7.4 %collective-permute-start.9 = (bf16[256,1,1024]{0,2,1:T(8,128)(2,1)S(1)}, bf16[256,1,1024]{0,2,1:T(8,128)(2,1)S(1)}, u32[]{:S(2)}, u32[]{:S(2)}) collective-permute-start(bf16[256,1,1024]{0,2,1:T(8,128)(2,1)S(1)} %collective-permute-done.8), channel_id=1, source_target_pairs={{0,1},{1,2},{2,3},{3,4},{4,5},{5,6},{6,7},{7,8},{8,9},{9,10},{10,1... | collective-permute-start | bytes 1572872 | tf_op jit(solution)/shard_map/ppermute | solution.py:18
  109.3 2.4 collective-permute-done.10
  115.5 6.5 %collective-permute-done.9 = bf16[256,1,1024]{0,2,1:T(8,128)(2,1)S(1)} collective-permute-done((bf16[256,1,1024]{0,2,1:T(8,128)(2,1)S(1)}, bf16[256,1,1024]{0,2,1:T(8,128)(2,1)S(1)}, u32[]{:S(2)}, u32[]{:S(2)}) %collective-permute-start.9) | collective-permute-done | bytes 524320 | tf_op jit(solution)/shard_map/ppermute | solution.py:18
  122.1 1.3 constant_dynamic-update-slice_fusion.3
  130.7 6.8 %copy.82 = bf16[256,16,6,6,64]{0,4,3,2,1:T(8,128)(2,1)} copy(bf16[256,16,6,6,64]{0,4,1,2,3:T(8,128)(2,1)S(1)} %bitcast.236) | data formatting | bytes 37748736 | tf_op jit(solution)/shard_map/transpose | solution.py:29
  137.5 11.4 %collective-permute-done.7 = bf16[256,2,1024]{0,2,1:T(8,128)(2,1)S(1)} collective-permute-done((bf16[256,2,1024]{0,2,1:T(8,128)(2,1)S(1)}, bf16[256,2,1024]{0,2,1:T(8,128)(2,1)S(1)}, u32[]{:S(2)}, u32[]{:S(2)}) %collective-permute-start.7) | collective-permute-done | bytes 1048608 | tf_op jit(solution)/shard_map/ppermute | solution.py:18
  152.6 6.8 %copy.91 = bf16[256,16,6,6,64]{0,4,3,2,1:T(8,128)(2,1)} copy(bf16[256,16,6,6,64]{0,4,1,2,3:T(8,128)(2,1)S(1)} %bitcast.237) | data formatting | bytes 37748736 | tf_op jit(solution)/shard_map/transpose | solution.py:29
  159.4 24.1 %fusion.77 = f32[16,64,2304]{2,1,0:T(8,128)} fusion(bf16[256,16,2304]{0,2,1:T(8,128)(2,1)} %bitcast.233, bf16[1,1,16,64,2304]{4,3,2,1,0:T(8,128)(2,1)} %param.7, bf16[4,1,16,64,256]{4,3,2,1,0:T(8,128)(2,1)} %param.11, s32[]{:T(128)S(6)} %select_n.56), kind=kOutput, calls=%fused_computation.84 | convolution fusion | flops 2417754112 | bytes 52428804 | tf_op jit(solution)/shard_map/cob,bck->cok/dot_general | solution.py:64
  183.5 24.2 %fusion.82 = f32[16,64,2304]{2,1,0:T(8,128)} fusion(bf16[256,16,2304]{0,2,1:T(8,128)(2,1)} %bitcast.234, bf16[1,1,16,64,2304]{4,3,2,1,0:T(8,128)(2,1)} %param.7, bf16[4,1,16,64,256]{4,3,2,1,0:T(8,128)(2,1)} %param.11, s32[]{:T(128)S(6)} %select_n.57), kind=kOutput, calls=%fused_computation.85 | convolution fusion | flops 2417754112 | bytes 52428804 | tf_op jit(solution)/shard_map/cob,bck->cok/dot_general | solution.py:64
  210.9 1.3 constant_dynamic-update-slice_fusion.25
  213.1 6.8 %copy.100 = bf16[256,16,6,6,64]{0,4,3,2,1:T(8,128)(2,1)} copy(bf16[256,16,6,6,64]{0,4,1,2,3:T(8,128)(2,1)S(1)} %bitcast.238) | data formatting | bytes 37748736 | tf_op jit(solution)/shard_map/transpose | solution.py:29
  219.9 25.6 %add_multiply_fusion = bf16[16,64,2304]{2,1,0:T(8,128)(2,1)} fusion(f32[16,64,2304]{2,1,0:T(8,128)} %fusion.77, f32[16,64,2304]{2,1,0:T(8,128)} %fusion.82, bf16[256,16,2304]{0,2,1:T(8,128)(2,1)} %bitcast.232, bf16[1,1,16,64,2304]{4,3,2,1,0:T(8,128)(2,1)} %param.7, bf16[4,1,16,64,256]{4,3,2,1,0:T(8,128)(2,1)} %param.11, s32[]{:T(128)S(6)} %select_n.58), kind=kOutput, calls=%fused_computation.2 | convolution fusion | flops 2427191296 | bytes 66584580 | tf_op jit(solution)/shard_map/cob,bck->cok/dot_general | solution.py:64
  245.4 5.3 %gather_fusion = bf16[4,4,64,2304]{3,2,1,0:T(8,128)(2,1)} fusion(bf16[4,4,64,2304]{3,2,1,0:T(8,128)(2,1)} %bitcast.235, s32[1024]{0:T(1024)S(1)} %pad_clamp_fusion.1), kind=kCustom, calls=%fused_computation | custom fusion | bytes 9437200 | tf_op jit(solution)/shard_map/jit(_take)/gather | solution.py:68
  250.8 5.6 %select_convert_fusion = bf16[4,4,64,2304]{3,2,1,0:T(8,128)(2,1)} fusion(bf16[4,4,64,2304]{3,2,1,0:T(8,128)(2,1)} %gather_fusion, pred[4]{0:T(512)(128)(4,1)S(1)} %compare_and_fusion), kind=kLoop, calls=%fused_computation.3 | loop fusion | flops 2359296 | bytes 9437188 | tf_op jit(solution)/shard_map/convert_element_type | solution.py:68
  256.4 54.8 %reduce-scatter.2.cloned.1.call-done = bf16[1,4,64,2304]{3,2,1,0:T(8,128)(2,1)} async-done(((bf16[4,4,64,2304]{3,2,1,0:T(8,128)(2,1)}), bf16[1,4,64,2304]{3,2,1,0:T(8,128)(2,1)}) %reduce-scatter.2.cloned.1.call-update) | async-done | bytes 1179664 | tf_op jit(solution)/shard_map/reduce_scatter | solution.py:69
  311.2 5.8 %fusion.110 = (bf16[1,1,4,64,2304]{4,3,2,1,0:T(8,128)(2,1)}, f32[1,1,4,64,2304]{4,3,2,1,0:T(8,128)}, f32[1,1,4,64,2304]{4,3,2,1,0:T(8,128)}) fusion(f32[1,1,4,64,2304]{4,3,2,1,0:T(8,128)S(1)} %copy-done.15, bf16[1,4,64,2304]{3,2,1,0:T(8,128)(2,1)} %reduce-scatter.2.cloned.1.call-done, f32[1,1,4,64,2304]{4,3,2,1,0:T(8,128)} %param.9), kind=kLoop, calls=%fused_computation.151 | loop fusion | flops 4718592 | bytes 11796480 | tf_op jit(solution)/shard_map/convert_element_type | solution.py:74
  317.3 51.8 %all-gather.3.cloned.1.call-done = bf16[4,1,4,64,2304]{4,3,2,1,0:T(8,128)(2,1)} async-done(((bf16[1,1,4,64,2304]{4,3,2,1,0:T(8,128)(2,1)}), bf16[4,1,4,64,2304]{4,3,2,1,0:T(8,128)(2,1)}) %all-gather.3.cloned.1.call-update) | async-done | bytes 4718608 | tf_op jit(solution)/shard_map/all_gather | solution.py:74
  369.1 5.4 %gather_fusion.1 = bf16[4,4,64,2304]{3,2,1,0:T(8,128)(2,1)} fusion(bf16[4,4,64,2304]{3,2,1,0:T(8,128)(2,1)} %bitcast.255, s32[1024]{0:T(1024)S(1)} %pad_clamp_fusion), kind=kCustom, calls=%fused_computation.1 | custom fusion | bytes 9437200 | tf_op jit(solution)/shard_map/jit(_take)/gather | solution.py:78
  374.5 5.0 %bitcast_select_fusion = bf16[1,16,64,2304]{3,2,1,0:T(8,128)(2,1)} fusion(pred[16]{0:T(512)(128)(4,1)S(1)} %broadcast_in_dim.31, bf16[1,16,64,2304]{3,2,1,0:T(8,128)(2,1)} %bitcast.239), kind=kLoop, calls=%fused_computation.4 | loop fusion | flops 2359296 | bytes 9437200 | tf_op jit(solution)/shard_map/jit(_take)/select_n | solution.py:78
  (114 shorter events, 21.9 us)
Async XLA Ops:
  7.2 27.5 %copy-start.20 = (s32[4]{0:T(128)S(1)}, s32[4]{0:T(128)}, u32[]{:S(2)}) copy-start(s32[4]{0:T(128)} %param.13) | copy-start | bytes 52
  7.2 304.0 %reduce-scatter.2.cloned.1.call-start = ((), (), s32[]{:S(2)}) async-start(), calls=%async_computation.1 | async-start | bytes 5898240 | tf_op jit(solution)/shard_map/reduce_scatter | solution.py:69
  16.0 99.4 %copy-start.7 = (bf16[1,256,1,1024]{1,3,2,0:T(8,128)(2,1)}, bf16[1,256,1,1024]{1,3,2,0:T(8,128)(2,1)S(1)}, u32[]{:S(2)}) copy-start(bf16[1,256,1,1024]{1,3,2,0:T(8,128)(2,1)S(1)} %copy.109) | copy-start | bytes 1572868
  16.0 38.7 %collective-permute-start = (bf16[256,1,1024]{0,2,1:T(8,128)(2,1)S(1)}, bf16[256,1,1024]{0,2,1:T(8,128)(2,1)}, u32[]{:S(2)}, u32[]{:S(2)}) collective-permute-start(bf16[256,1,1024]{0,2,1:T(8,128)(2,1)S(1)} %bitcast.250), channel_id=1, source_target_pairs={{0,1},{1,2},{2,3},{3,4},{4,5},{5,6},{6,7},{7,8},{8,9},{9,10},{10,1... | collective-permute-start | bytes 1572872 | tf_op jit(solution)/shard_map/ppermute | solution.py:18
  18.9 47.9 %collective-permute-start.2 = (bf16[256,1,1024]{0,2,1:T(8,128)(2,1)S(1)}, bf16[256,1,1024]{0,2,1:T(8,128)(2,1)S(1)}, u32[]{:S(2)}, u32[]{:S(2)}) collective-permute-start(bf16[256,1,1024]{0,2,1:T(8,128)(2,1)S(1)} %bitcast.251), channel_id=1, source_target_pairs={{1,0},{2,1},{3,2},{4,3},{5,4},{6,5},{7,6},{8,7},{9,8},{10,9},{11,1... | collective-permute-start | bytes 1572872 | tf_op jit(solution)/shard_map/ppermute | solution.py:18
  23.8 91.7 %copy-start.5 = (bf16[1,256,1,1024]{1,3,2,0:T(8,128)(2,1)}, bf16[1,256,1,1024]{1,3,2,0:T(8,128)(2,1)S(1)}, u32[]{:S(2)}) copy-start(bf16[1,256,1,1024]{1,3,2,0:T(8,128)(2,1)S(1)} %copy.110) | copy-start | bytes 1572868
  23.8 53.4 %collective-permute-start.4 = (bf16[256,1,1024]{0,2,1:T(8,128)(2,1)S(1)}, bf16[256,1,1024]{0,2,1:T(8,128)(2,1)}, u32[]{:S(2)}, u32[]{:S(2)}) collective-permute-start(bf16[256,1,1024]{0,2,1:T(8,128)(2,1)S(1)} %bitcast.245), channel_id=1, source_target_pairs={{0,1},{1,2},{2,3},{3,4},{4,5},{5,6},{6,7},{7,8},{8,9},{9,10},{10,1... | collective-permute-start | bytes 1572872 | tf_op jit(solution)/shard_map/ppermute | solution.py:18
  26.8 73.7 %collective-permute-start.6 = (bf16[256,1,1024]{0,2,1:T(8,128)(2,1)S(1)}, bf16[256,1,1024]{0,2,1:T(8,128)(2,1)S(1)}, u32[]{:S(2)}, u32[]{:S(2)}) collective-permute-start(bf16[256,1,1024]{0,2,1:T(8,128)(2,1)S(1)} %bitcast.246), channel_id=1, source_target_pairs={{1,0},{2,1},{3,2},{4,3},{5,4},{6,5},{7,6},{8,7},{9,8},{10,9},{11,1... | collective-permute-start | bytes 1572872 | tf_op jit(solution)/shard_map/ppermute | solution.py:18
  31.6 90.4 %copy-start.2 = (bf16[1,256,1,1024]{1,3,2,0:T(8,128)(2,1)}, bf16[1,256,1,1024]{1,3,2,0:T(8,128)(2,1)S(1)}, u32[]{:S(2)}) copy-start(bf16[1,256,1,1024]{1,3,2,0:T(8,128)(2,1)S(1)} %copy.111) | copy-start | bytes 1572868
  31.6 70.2 %collective-permute-start.8 = (bf16[256,1,1024]{0,2,1:T(8,128)(2,1)S(1)}, bf16[256,1,1024]{0,2,1:T(8,128)(2,1)S(1)}, u32[]{:S(2)}, u32[]{:S(2)}) collective-permute-start(bf16[256,1,1024]{0,2,1:T(8,128)(2,1)S(1)} %bitcast.240), channel_id=1, source_target_pairs={{0,1},{1,2},{2,3},{3,4},{4,5},{5,6},{6,7},{7,8},{8,9},{9,10},{10,1... | collective-permute-start | bytes 1572872 | tf_op jit(solution)/shard_map/ppermute | solution.py:18
  54.7 57.0 %collective-permute-start.10 = (bf16[256,1,1024]{0,2,1:T(8,128)(2,1)S(1)}, bf16[256,1,1024]{0,2,1:T(8,128)(2,1)S(1)}, u32[]{:S(2)}, u32[]{:S(2)}) collective-permute-start(bf16[256,1,1024]{0,2,1:T(8,128)(2,1)S(1)} %bitcast.241), channel_id=1, source_target_pairs={{1,0},{2,1},{3,2},{4,3},{5,4},{6,5},{7,6},{8,7},{9,8},{10,9},{11,1... | collective-permute-start | bytes 1572872 | tf_op jit(solution)/shard_map/ppermute | solution.py:18
  66.8 55.3 %copy-start.13 = (bf16[256,1,1024]{0,2,1:T(8,128)(2,1)}, bf16[256,1,1024]{0,2,1:T(8,128)(2,1)S(1)}, u32[]{:S(2)}) copy-start(bf16[256,1,1024]{0,2,1:T(8,128)(2,1)S(1)} %collective-permute-done.2) | copy-start | bytes 1572868
  66.8 47.3 %collective-permute-start.1 = (bf16[256,1,1024]{0,2,1:T(8,128)(2,1)}, bf16[256,1,1024]{0,2,1:T(8,128)(2,1)S(1)}, u32[]{:S(2)}, u32[]{:S(2)}) collective-permute-start(bf16[256,1,1024]{0,2,1:T(8,128)(2,1)} %collective-permute-done), channel_id=1, source_target_pairs={{0,1},{1,2},{2,3},{3,4},{4,5},{5,6},{6,7},{7,8},{8,9},{9,10},{10,1... | collective-permute-start | bytes 1572872 | tf_op jit(solution)/shard_map/ppermute | solution.py:18
  77.2 38.2 %collective-permute-start.5 = (bf16[256,1,1024]{0,2,1:T(8,128)(2,1)}, bf16[256,1,1024]{0,2,1:T(8,128)(2,1)S(1)}, u32[]{:S(2)}, u32[]{:S(2)}) collective-permute-start(bf16[256,1,1024]{0,2,1:T(8,128)(2,1)} %collective-permute-done.4), channel_id=1, source_target_pairs={{0,1},{1,2},{2,3},{3,4},{4,5},{5,6},{6,7},{7,8},{8,9},{9,10},{10,1... | collective-permute-start | bytes 1572872 | tf_op jit(solution)/shard_map/ppermute | solution.py:18
  100.5 21.6 %copy-start.11 = (bf16[256,1,1024]{0,2,1:T(8,128)(2,1)}, bf16[256,1,1024]{0,2,1:T(8,128)(2,1)S(1)}, u32[]{:S(2)}) copy-start(bf16[256,1,1024]{0,2,1:T(8,128)(2,1)S(1)} %collective-permute-done.6) | copy-start | bytes 1572868
  100.5 26.5 %collective-permute-start.3 = (bf16[256,2,1024]{0,2,1:T(8,128)(2,1)S(1)}, bf16[256,2,1024]{0,2,1:T(8,128)(2,1)S(1)}, u32[]{:S(2)}, u32[]{:S(2)}) collective-permute-start(bf16[256,2,1024]{0,2,1:T(8,128)(2,1)S(1)} %pad_maximum_fusion), channel_id=1, source_target_pairs={{2,0},{3,1},{4,2},{5,3},{6,4},{7,5},{8,6},{9,7},{10,8},{11,9},{12,... | collective-permute-start | bytes 3145736 | tf_op jit(solution)/shard_map/ppermute | solution.py:18
  101.8 25.1 %copy-start.16 = (bf16[256,1,1024]{0,2,1:T(8,128)(2,1)}, bf16[256,1,1024]{0,2,1:T(8,128)(2,1)S(1)}, u32[]{:S(2)}) copy-start(bf16[256,1,1024]{0,2,1:T(8,128)(2,1)S(1)} %collective-permute-done.8) | copy-start | bytes 1572868
  101.8 20.2 %collective-permute-start.9 = (bf16[256,1,1024]{0,2,1:T(8,128)(2,1)S(1)}, bf16[256,1,1024]{0,2,1:T(8,128)(2,1)S(1)}, u32[]{:S(2)}, u32[]{:S(2)}) collective-permute-start(bf16[256,1,1024]{0,2,1:T(8,128)(2,1)S(1)} %collective-permute-done.8), channel_id=1, source_target_pairs={{0,1},{1,2},{2,3},{3,4},{4,5},{5,6},{6,7},{7,8},{8,9},{9,10},{10,1... | collective-permute-start | bytes 1572872 | tf_op jit(solution)/shard_map/ppermute | solution.py:18
  111.7 15.2 %copy-start.9 = (bf16[256,1,1024]{0,2,1:T(8,128)(2,1)}, bf16[256,1,1024]{0,2,1:T(8,128)(2,1)S(1)}, u32[]{:S(2)}) copy-start(bf16[256,1,1024]{0,2,1:T(8,128)(2,1)S(1)} %collective-permute-done.10) | copy-start | bytes 1572868
  111.7 37.2 %collective-permute-start.7 = (bf16[256,2,1024]{0,2,1:T(8,128)(2,1)S(1)}, bf16[256,2,1024]{0,2,1:T(8,128)(2,1)S(1)}, u32[]{:S(2)}, u32[]{:S(2)}) collective-permute-start(bf16[256,2,1024]{0,2,1:T(8,128)(2,1)S(1)} %pad_maximum_fusion.1), channel_id=1, source_target_pairs={{2,0},{3,1},{4,2},{5,3},{6,4},{7,5},{8,6},{9,7},{10,8},{11,9},{12,... | collective-permute-start | bytes 3145736 | tf_op jit(solution)/shard_map/ppermute | solution.py:18
  114.0 93.7 %collective-permute-start.11 = (bf16[256,2,1024]{0,2,1:T(8,128)(2,1)}, bf16[256,2,1024]{0,2,1:T(8,128)(2,1)}, u32[]{:S(2)}, u32[]{:S(2)}) collective-permute-start(bf16[256,2,1024]{0,2,1:T(8,128)(2,1)} %pad_maximum_fusion.2), channel_id=1, source_target_pairs={{2,0},{3,1},{4,2},{5,3},{6,4},{7,5},{8,6},{9,7},{10,8},{11,9},{12,... | collective-permute-start | bytes 3145736 | tf_op jit(solution)/shard_map/ppermute | solution.py:18
  122.0 4.9 %copy-start.18 = (bf16[256,1,1024]{0,2,1:T(8,128)(2,1)}, bf16[256,1,1024]{0,2,1:T(8,128)(2,1)S(1)}, u32[]{:S(2)}) copy-start(bf16[256,1,1024]{0,2,1:T(8,128)(2,1)S(1)} %collective-permute-done.9) | copy-start | bytes 1572868
  122.0 4.7 %copy-start.6 = (bf16[1,256,1,1024]{1,3,2,0:T(8,128)(2,1)S(1)}, bf16[1,256,1,1024]{1,3,2,0:T(8,128)(2,1)}, u32[]{:S(2)}) copy-start(bf16[1,256,1,1024]{1,3,2,0:T(8,128)(2,1)} %copy-done.5) | copy-start | bytes 1572868
  122.0 4.7 %copy-start.12 = (bf16[256,1,1024]{0,2,1:T(8,128)(2,1)S(1)}, bf16[256,1,1024]{0,2,1:T(8,128)(2,1)}, u32[]{:S(2)}) copy-start(bf16[256,1,1024]{0,2,1:T(8,128)(2,1)} %copy-done.11) | copy-start | bytes 1572868
  122.0 4.8 %copy-start.3 = (bf16[1,256,1,1024]{1,3,2,0:T(8,128)(2,1)S(1)}, bf16[1,256,1,1024]{1,3,2,0:T(8,128)(2,1)}, u32[]{:S(2)}) copy-start(bf16[1,256,1,1024]{1,3,2,0:T(8,128)(2,1)} %copy-done.2) | copy-start | bytes 1572868
  127.6 1.6 copy-start.8
  127.6 1.6 copy-start.14
  209.4 1.3 copy-start.4
  209.4 1.5 copy-start.10
  256.4 54.8 %copy-start.15 = (f32[1,1,4,64,2304]{4,3,2,1,0:T(8,128)S(1)}, f32[1,1,4,64,2304]{4,3,2,1,0:T(8,128)}, u32[]{:S(2)}) copy-start(f32[1,1,4,64,2304]{4,3,2,1,0:T(8,128)} %param.8) | copy-start | bytes 7077892
  256.4 112.7 %all-gather.3.cloned.1.call-start = ((), (), s32[]{:S(2)}) async-start(), calls=%async_computation.2 | async-start | bytes 5898240 | tf_op jit(solution)/shard_map/all_gather | solution.py:74
  374.5 5.1 %copy-start.1 = (s32[4,3]{1,0:T(4,128)S(1)}, s32[4,3]{1,0:T(4,128)}, u32[]{:S(2)}) copy-start(s32[4,3]{1,0:T(4,128)} %param.12) | copy-start | bytes 148
  (3 other events, 2.9 us)
Sparse Core Ops, SparseCore 0:
  256.5 54.6 reduce-scatter.1
  317.1 51.9 all-gather.2
where the time goes:
time: 389 us; the launch traced here: 386 us
  waiting for transfers between devices  185 us (48%)
  matrix products  74 us (19%)
  local copies, waits for them, and re-layouts  51.8 us (13%)
  starting transfers between devices  37.5 us (10%)
  between operations  20.6 us (5%)
  other arithmetic  17.8 us (5%)
    ppermute x12, waiting for transfers between devices, passed_along(): return lax.ppermute(shard, axis, pairs)  78.1 us
    dot_general x3, matrix products, per_device(): jnp.einsum('cob,bck->cok', signal, patches, preferred_element_type=jnp.fl...  74 us
    reduce_scatter x1, waiting for transfers between devices, per_device(): lax.psum_scatter(ordered, 'rep', scatter_dimension=0, tiled=True)  54.8 us
    all_gather x1, waiting for transfers between devices, per_device(): lax.all_gather(master_next[0].astype(jnp.bfloat16), 'rep', axis=0, tiled=...  51.8 us
    ppermute x12, starting transfers between devices, passed_along(): return lax.ppermute(shard, axis, pairs)  37.4 us
    transpose x3, local copies, waits for them, and re-layouts, build_patches(): stacked.transpose(0, 3, 1, 2, 4)  20.4 us
    unnamed x84, local copies, waits for them, and re-layouts  15.9 us
  transfers between devices with their start and end apart: 14, of which 9 were waited for; matrix products, arithmetic and copies ran while one was open for 20% of the time, Pallas kernels for 0%

commit v1 on v0

v1 whole, which is shorter than its diff:
```python
import functools

import jax
import jax.numpy as jnp
from jax import lax
from jax.experimental import pallas as pl
from jax.experimental.pallas import tpu as pltpu
from jax.sharding import PartitionSpec as P

MICRO = 3
POOL = 4
FIELD = 6
REPS = 4
CB = 4
CH = 64
MAPS = 64
TAPS = FIELD * CH
BAND = 640
LEFT = 128
HALVES = 2
OWN = 2
FACTOR = (FIELD * FIELD * CH) ** (-0.5)
LEARNING_RATE = 0.3
EPSILON = 1e-08

MESH = pl.DeviceIdType.MESH


def step_kernel(
    sites,
    pick_ref,
    count_ref,
    images_ref,
    targets_ref,
    working_ref,
    master_ref,
    accum_ref,
    fetched_ref,
    master_out,
    accum_out,
    x0,
    x1,
    x2,
    x3,
    x4,
    x5,
    weights,
    banded,
    targets,
    signal,
    chosen,
    chosen_in,
    kept,
    own,
    pair,
    pair_in,
    combined,
    window,
    master,
    accum,
    mine,
    theirs,
    grad,
    sem_load,
    send_a,
    send_b,
    send_c,
    send_d,
    send_e,
    send_f,
    send_g,
    send_x,
    recv_l,
    recv_x,
    send_s,
    recv_s,
    send_p,
    recv_p,
    send_w,
    recv_w,
    sem_store,
):
    x = [x0, x1, x2, x3, x4, x5]
    batch = images_ref.shape[1]
    width = images_ref.shape[2]
    piece = batch // HALVES
    duo = 2 * piece
    span = POOL * piece

    g = lax.axis_index("rep")
    s = lax.axis_index("site")
    side = g // 2
    core = g % 2
    odd = s % 2
    even = odd == 0

    def peer(k):
        return 2 * ((side + k // 2) % 2) + (core + k % 2) % 2

    ahead = (g, s + 2)
    behind = (g, s - 2)
    across = (2 * (1 - side) + core, s + 1 - 2 * odd)
    partner = (2 * (1 - side) + core, s)
    sibling = (2 * side + 1 - core, s)
    has_ahead = s + 2 < sites
    has_behind = s >= 2
    valid = [(s + d - 2 >= 0) & (s + d - 2 < sites) for d in range(FIELD)]
    halves = range(HALVES)

    def own_image(p, h):
        return pltpu.make_async_copy(
            images_ref.at[p, pl.ds(h * piece, piece)],
            x[OWN].at[pl.ds(h * span + p * piece, piece), pl.ds(LEFT, width)],
            sem_load.at[p, h],
        )

    loads = [
        pltpu.make_async_copy(working_ref, weights, sem_load.at[POOL, 0]),
        pltpu.make_async_copy(targets_ref, targets, sem_load.at[POOL + 1, 0]),
        pltpu.make_async_copy(master_ref, master, sem_load.at[POOL + 2, 0]),
        pltpu.make_async_copy(accum_ref, accum, sem_load.at[POOL + 3, 0]),
    ]
    for h in halves:
        for p in range(POOL):
            own_image(p, h).start()
    for load in loads:
        load.start()

    right = x[0].shape[1] - LEFT - width
    for d in range(FIELD):
        x[d][:, 0:LEFT] = jnp.zeros((POOL * batch, LEFT), jnp.bfloat16)
        x[d][:, LEFT + width :] = jnp.zeros((POOL * batch, right), jnp.bfloat16)
        if d != OWN:

            @pl.when(jnp.logical_not(valid[d]))
            def _(d=d):
                x[d][:, LEFT : LEFT + width] = jnp.zeros((POOL * batch, width), jnp.bfloat16)

    barrier = pltpu.get_barrier_semaphore()
    for device in (across, partner, sibling):
        pl.semaphore_signal(barrier, inc=1, device_id=device, device_id_type=MESH)

    @pl.when(has_ahead)
    def _():
        pl.semaphore_signal(barrier, inc=1, device_id=ahead, device_id_type=MESH)

    @pl.when(has_behind)
    def _():
        pl.semaphore_signal(barrier, inc=1, device_id=behind, device_id_type=MESH)

    pl.semaphore_wait(barrier, 3 + has_ahead.astype(jnp.int32) + has_behind.astype(jnp.int32))

    q = (2 * core + side, 2 * core + 1 - side)

    def rows(slot, p, h):
        return x[slot].at[
            pl.ds(pl.multiple_of(h * span + p * piece, piece), piece), pl.ds(LEFT, width)
        ]

    def link(src, dst, p, h, device, sem):
        return pltpu.make_async_remote_copy(
            src_ref=rows(src, p, h),
            dst_ref=rows(dst, p, h),
            send_sem=sem,
            recv_sem=recv_l.at[dst, p % 2, h],
            device_id=device,
            device_id_type=MESH,
        )

    def hand_over(slot, p, h):
        return pltpu.make_async_remote_copy(
            src_ref=rows(slot, p, h),
            dst_ref=rows(slot, p, h),
            send_sem=send_x.at[slot, p % 2, h],
            recv_sem=recv_x.at[slot, p % 2, h],
            device_id=sibling,
            device_id_type=MESH,
        )

    def natives(h):
        for p in range(POOL):
            own_image(p, h).wait()

        @pl.when(has_ahead)
        def _():
            for i in (0, 1):
                link(OWN, 0, q[i], h, ahead, send_a.at[i, h]).start()

        @pl.when(has_behind)
        def _():
            for i in (1, 0):
                link(OWN, 4, q[i], h, behind, send_b.at[i, h]).start()

        @pl.when(even)
        def _():
            link(OWN, 1, q[0], h, across, send_c.at[0, h]).start()

            @pl.when(s == 0)
            def _():
                link(OWN, 1, q[1], h, across, send_c.at[1, h]).start()

        @pl.when(odd == 1)
        def _():
            for i in (1, 0):
                link(OWN, 3, q[i], h, across, send_c.at[i, h]).start()

    def passed(slot, p, h, *sends):
        @pl.when(valid[slot])
        def _():
            link(slot, slot, p, h, partner, send_a.at[0, 0]).wait_recv()
            for condition, copy in sends:

                @pl.when(condition)
                def _(copy=copy):
                    copy.start()

            hand_over(slot, p, h).start()

    def onward(h):
        return (
            (has_ahead, link(3, 1, q[0], h, ahead, send_e.at[h])),
            (has_behind, link(3, 5, q[0], h, behind, send_f.at[h])),
        )

    def swap(h):
        return (valid[5], link(5, 5, q[0], h, partner, send_g.at[h]))

    def arrivals_one(h):
        @pl.when(even)
        def _():
            passed(4, q[1], h, (has_ahead, link(4, 3, q[1], h, across, send_d.at[1, h])))
            passed(3, q[0], h, *onward(h))
            passed(0, q[0], h)

        @pl.when(odd == 1)
        def _():
            passed(0, q[0], h, (has_behind, link(0, 1, q[0], h, across, send_d.at[0, h])))
            passed(4, q[1], h)
            passed(1, q[1], h)

    def arrivals_two(h):
        @pl.when(even)
        def _():
            passed(4, q[0], h, (has_ahead, link(4, 3, q[0], h, across, send_d.at[0, h])))
            passed(3, q[1], h)
            passed(0, q[1], h)

        @pl.when(odd == 1)
        def _():
            passed(3, q[0], h, *onward(h))
            passed(4, q[0], h)
            passed(0, q[1], h)

    def arrivals_three(h):
        passed(5, q[0], h, swap(h))
        passed(1, q[0], h)

        @pl.when(even)
        def _():
            passed(1, q[1], h)

        @pl.when(odd == 1)
        def _():
            passed(3, q[1], h)

        passed(5, q[1], h)
        for slot in (0, 1, 3, 4, 5):

            @pl.when(valid[slot])
            def _(slot=slot):
                for j in range(2):
                    pltpu.make_async_remote_copy(
                        src_ref=rows(slot, 2 * (1 - core) + j, h),
                        dst_ref=rows(slot, 2 * (1 - core) + j, h),
                        send_sem=send_x.at[slot, j, h],
                        recv_sem=recv_x.at[slot, j, h],
                        device_id=sibling,
                        device_id_type=MESH,
                    ).wait_recv()

    def band_weights(block, carry):
        for cc in range(CB):
            for d in range(FIELD):
                taps = weights[block * CB + cc, :, d * TAPS : (d + 1) * TAPS]
                if cc % 2:
                    wide = jnp.concatenate(
                        [taps.astype(jnp.float32), jnp.zeros((MAPS, LEFT), jnp.float32)], axis=1
                    )
                    taps = pltpu.roll(wide, CH, 1).astype(jnp.bfloat16)
                before = (cc // 2) * LEFT
                after = BAND - before - taps.shape[1]
                parts = [taps]
                if before:
                    parts = [jnp.zeros((MAPS, before), jnp.bfloat16)] + parts
                if after:
                    parts = parts + [jnp.zeros((MAPS, after), jnp.bfloat16)]
                banded[block, cc * MAPS : (cc + 1) * MAPS, d * BAND : (d + 1) * BAND] = (
                    jnp.concatenate(parts, axis=1)
                )
        return carry

    def forward(h, n, low, high):
        at = h * span + n * duo

        def one_block(block, carry):
            lanes = pl.multiple_of(block * (CB * CH), CB * CH)
            total = jnp.zeros((CB * MAPS, duo), jnp.float32)
            for d in range(FIELD):
                total = total + lax.dot_general(
                    banded[block, :, d * BAND : (d + 1) * BAND],
                    x[d][at : at + duo, pl.ds(lanes, BAND)],
                    (((1,), (1,)), ((), ())),
                    preferred_element_type=jnp.float32,
                )
            active = jnp.tanh(FACTOR * total)
            of_block = pl.ds(pl.multiple_of(block * (CB * MAPS), CB * MAPS), CB * MAPS)
            of_half = slice(h * piece, (h + 1) * piece)
            wanted = jnp.concatenate(
                [targets[2 * n, of_block, of_half], targets[2 * n + 1, of_block, of_half]], axis=1
            ).astype(jnp.float32)
            signal[block] = ((active - wanted) * (1.0 - active * active)).astype(jnp.bfloat16)
            return carry

        lax.fori_loop(low, high, one_block, 0)

    strip = 32

    def select(h, n):
        def one_strip(i, carry):
            at = pl.ds(pl.multiple_of(i * strip, strip), strip)
            parts = [signal[block, at, :] for block in range(REPS)]
            results = []
            for k in range(REPS):
                taken = None
                for block in range(REPS):
                    scale = jnp.full((strip, duo), pick_ref[peer(k), block], jnp.float32)
                    term = scale.astype(jnp.bfloat16) * parts[block]
                    taken = term if taken is None else taken + term
                results.append(taken)
            own[h, n, at, :] = results[0]
            chosen[h, n, 0, at, :] = results[1]
            kept[h, n, at, :] = results[2]
            chosen[h, n, 1, at, :] = results[3]
            return carry

        lax.fori_loop(0, CB * MAPS // strip, one_strip, 0)

    def choice(h, n):
        return pltpu.make_async_remote_copy(
            src_ref=chosen.at[h, n],
            dst_ref=chosen_in.at[h, n],
            send_sem=send_s.at[h, n],
            recv_sem=recv_s.at[h, n],
            device_id=sibling,
            device_id_type=MESH,
        )

    def pair_copy(h, n):
        return pltpu.make_async_remote_copy(
            src_ref=pair.at[h, n],
            dst_ref=pair_in.at[h, n],
            send_sem=send_p.at[h, n],
            recv_sem=recv_p.at[h, n],
            device_id=partner,
            device_id_type=MESH,
        )

    def weighed(k, n, value):
        value = value.astype(jnp.float32)
        return jnp.concatenate(
            [
                count_ref[peer(k), 2 * n] * value[:, :piece],
                count_ref[peer(k), 2 * n + 1] * value[:, piece:],
            ],
            axis=1,
        )

    def make_pair(h, n):
        choice(h, n).wait_recv()

        def one_strip(i, carry):
            at = pl.ds(pl.multiple_of(i * strip, strip), strip)
            pair[h, n, at, :] = (
                weighed(0, n, kept[h, n, at, :]) + weighed(1, n, chosen_in[h, n, 1, at, :])
            ).astype(jnp.bfloat16)
            return carry

        lax.fori_loop(0, CB * MAPS // strip, one_strip, 0)
        pair_copy(h, n).start()

    def combine(h, n):
        pair_copy(h, n).wait_recv()
        lanes = slice(h * span + n * duo, h * span + (n + 1) * duo)

        def one_strip(i, carry):
            at = pl.ds(pl.multiple_of(i * strip, strip), strip)
            combined[at, lanes] = (
                weighed(0, n, own[h, n, at, :])
                + weighed(1, n, chosen_in[h, n, 0, at, :])
                + pair_in[h, n, at, :].astype(jnp.float32)
            ).astype(jnp.bfloat16)
            return carry

        lax.fori_loop(0, CB * MAPS // strip, one_strip, 0)

    def own_window(h):
        def one_strip(i, carry):
            at = pl.ds(pl.multiple_of(h * span + i * strip, strip), strip)
            for d in range(FIELD):
                taken = None
                for block in range(REPS):
                    scale = jnp.full((strip, BAND), pick_ref[g, block], jnp.float32)
                    lanes = slice(block * CB * CH, block * CB * CH + BAND)
                    term = scale.astype(jnp.bfloat16) * x[d][at, lanes]
                    taken = term if taken is None else taken + term
                window[d, at, :] = taken
            return carry

        lax.fori_loop(0, span // strip, one_strip, 0)

    natives(0)
    loads[0].wait()
    lax.fori_loop(0, REPS, band_weights, 0)
    for load in loads[1:]:
        load.wait()
    arrivals_one(0)
    arrivals_two(0)
    natives(1)
    arrivals_three(0)
    forward(0, 0, 0, REPS)
    select(0, 0)
    choice(0, 0).start()
    arrivals_one(1)
    forward(0, 1, 0, REPS)
    make_pair(0, 0)
    select(0, 1)
    choice(0, 1).start()
    arrivals_two(1)
    make_pair(0, 1)
    own_window(0)
    combine(0, 0)
    combine(0, 1)
    arrivals_three(1)
    forward(1, 0, 0, REPS)
    select(1, 0)
    choice(1, 0).start()
    forward(1, 1, 0, REPS // 2)
    make_pair(1, 0)
    forward(1, 1, REPS // 2, REPS)
    select(1, 1)
    choice(1, 1).start()
    own_window(1)
    make_pair(1, 1)
    combine(1, 0)
    combine(1, 1)

    def part_of(ref, d):
        return ref.at[:, :, pl.ds(d * TAPS, TAPS)]

    def send_across(d):
        return pltpu.make_async_remote_copy(
            src_ref=part_of(mine, d),
            dst_ref=part_of(theirs, d),
            send_sem=send_w.at[0, d],
            recv_sem=recv_w.at[0, d],
            device_id=partner,
            device_id_type=MESH,
        )

    def send_beside(d):
        return pltpu.make_async_remote_copy(
            src_ref=part_of(mine, d),
            dst_ref=part_of(fetched_ref.at[1], d),
            send_sem=send_w.at[1, d],
            recv_sem=recv_w.at[1, d],
            device_id=sibling,
            device_id_type=MESH,
        )

    def pass_beside(d):
        return pltpu.make_async_remote_copy(
            src_ref=part_of(theirs, d),
            dst_ref=part_of(fetched_ref.at[3], d),
            send_sem=send_w.at[2, d],
            recv_sem=recv_w.at[2, d],
            device_id=sibling,
            device_id_type=MESH,
        )

    def stores(d):
        return [
            pltpu.make_async_copy(
                part_of(mine, d), part_of(fetched_ref.at[0], d), sem_store.at[0, d]
            ),
            pltpu.make_async_copy(part_of(master, d), part_of(master_out, d), sem_store.at[1, d]),
            pltpu.make_async_copy(part_of(accum, d), part_of(accum_out, d), sem_store.at[2, d]),
        ]

    def store_theirs(d):
        return pltpu.make_async_copy(
            part_of(theirs, d), part_of(fetched_ref.at[2], d), sem_store.at[3, d]
        )

    def send_part(d):
        send_across(d).start()
        send_beside(d).start()
        for store in stores(d):
            store.start()

    for d in range(FIELD):
        for at in range(0, BAND, 256):
            wide = min(256, BAND - at)
            grad[:, at : at + wide] = jnp.dot(
                combined[...],
                window[d, :, at : at + wide],
                preferred_element_type=jnp.float32,
            )
        if d:
            send_part(d - 1)
        for cc in range(CB):
            before = (cc // 2) * LEFT
            of_column = slice(cc * MAPS, (cc + 1) * MAPS)
            if cc % 2:
                wide = grad[of_column, before : before + TAPS + LEFT]
                column = pltpu.roll(wide, TAPS + LEFT - CH, 1)[:, :TAPS]
            else:
                column = grad[of_column, before : before + TAPS]
            slot_grad = FACTOR * column
            taps = slice(d * TAPS, (d + 1) * TAPS)
            accum_next = accum[cc, :, taps] + slot_grad * slot_grad
            master_next = master[cc, :, taps] - LEARNING_RATE * slot_grad / (
                jnp.sqrt(accum_next) + EPSILON
            )
            accum[cc, :, taps] = accum_next
            master[cc, :, taps] = master_next
            mine[cc, :, taps] = master_next.astype(jnp.bfloat16)

    send_part(FIELD - 1)
    for d in range(FIELD):
        send_across(d).wait_recv()
        pass_beside(d).start()
        store_theirs(d).start()

    for d in range(FIELD):
        send_across(d).wait_send()
        send_beside(d).wait()
        for store in stores(d):
            store.wait()
        store_theirs(d).wait()
        pass_beside(d).wait()
    for h in halves:
        for n in range(POOL // 2):
            choice(h, n).wait_send()
            pair_copy(h, n).wait_send()

    def all_sent(condition, sems):
        @pl.when(condition)
        def _():
            for sem in sems:
                link(OWN, OWN, 0, 0, partner, sem).wait_send()

    all_sent(has_ahead, [send_a.at[i, h] for i in (0, 1) for h in halves])
    all_sent(has_behind, [send_b.at[i, h] for i in (0, 1) for h in halves])
    all_sent(s >= 0, [send_c.at[0, h] for h in halves])
    all_sent((odd == 1) | (s == 0), [send_c.at[1, h] for h in halves])
    all_sent((even & has_ahead) | ((odd == 1) & has_behind), [send_d.at[0, h] for h in halves])
    all_sent(even & has_ahead, [send_d.at[1, h] for h in halves])
    all_sent(has_ahead, [send_e.at[h] for h in halves])
    all_sent(has_behind & valid[3], [send_f.at[h] for h in halves])
    all_sent(valid[5], [send_g.at[h] for h in halves])
    for slot in (0, 1, 3, 4, 5):
        all_sent(valid[slot], [send_x.at[slot, j, h] for j in (0, 1) for h in halves])


def per_device(
    working, master_slots, accum_slots, pool_images, pool_targets, batch_index, owner_map
):
    sites = lax.axis_size("site")
    batch = pool_images.shape[1]
    width = pool_images.shape[3]
    weights = working[0, 0]
    columns, maps, kdim = weights.shape
    padded = width - CB * CH + BAND
    duo = 2 * (batch // HALVES)
    me = lax.axis_index("rep")
    numbers = jnp.arange(REPS, dtype=jnp.int32)
    pick = (owner_map[:, None] == numbers).astype(jnp.float32)
    count = jnp.sum((batch_index[:, :, None] == numbers).astype(jnp.float32), axis=1)
    any_space = pl.BlockSpec(memory_space=pl.ANY)
    smem = pl.BlockSpec(memory_space=pltpu.SMEM)
    dma = pltpu.SemaphoreType.DMA
    fetched, master_next, accum_next = pl.pallas_call(
        functools.partial(step_kernel, sites),
        out_shape=(
            jax.ShapeDtypeStruct((REPS, CB, maps, kdim), jnp.bfloat16),
            jax.ShapeDtypeStruct((CB, maps, kdim), jnp.float32),
            jax.ShapeDtypeStruct((CB, maps, kdim), jnp.float32),
        ),
        in_specs=[smem, smem] + [any_space] * 5,
        out_specs=(any_space, any_space, any_space),
        scratch_shapes=[pltpu.VMEM((POOL * batch, padded), jnp.bfloat16)] * FIELD
        + [
            pltpu.VMEM((columns, maps, kdim), jnp.bfloat16),
            pltpu.VMEM((REPS, CB * maps, FIELD * BAND), jnp.bfloat16),
            pltpu.VMEM((POOL, columns * maps, batch), jnp.bfloat16),
            pltpu.VMEM((REPS, CB * maps, duo), jnp.bfloat16),
            pltpu.VMEM((HALVES, 2, 2, CB * maps, duo), jnp.bfloat16),
            pltpu.VMEM((HALVES, 2, 2, CB * maps, duo), jnp.bfloat16),
            pltpu.VMEM((HALVES, 2, CB * maps, duo), jnp.bfloat16),
            pltpu.VMEM((HALVES, 2, CB * maps, duo), jnp.bfloat16),
            pltpu.VMEM((HALVES, 2, CB * maps, duo), jnp.bfloat16),
            pltpu.VMEM((HALVES, 2, CB * maps, duo), jnp.bfloat16),
            pltpu.VMEM((CB * maps, POOL * batch), jnp.bfloat16),
            pltpu.VMEM((FIELD, POOL * batch, BAND), jnp.bfloat16),
            pltpu.VMEM((CB, maps, kdim), jnp.float32),
            pltpu.VMEM((CB, maps, kdim), jnp.float32),
            pltpu.VMEM((CB, maps, kdim), jnp.bfloat16),
            pltpu.VMEM((CB, maps, kdim), jnp.bfloat16),
            pltpu.VMEM((CB * maps, BAND), jnp.float32),
            dma((POOL + 4, HALVES)),
            dma((2, HALVES)),
            dma((2, HALVES)),
            dma((2, HALVES)),
            dma((2, HALVES)),
            dma((HALVES,)),
            dma((HALVES,)),
            dma((HALVES,)),
            dma((FIELD, 2, HALVES)),
            dma((FIELD, 2, HALVES)),
            dma((FIELD, 2, HALVES)),
            dma((HALVES, 2)),
            dma((HALVES, 2)),
            dma((HALVES, 2)),
            dma((HALVES, 2)),
            dma((3, FIELD)),
            dma((3, FIELD)),
            dma((4, FIELD)),
        ],
        compiler_params=pltpu.CompilerParams(
            collective_id=0, has_side_effects=True, vmem_limit_bytes=62 * 1024 * 1024
        ),
        name="step",
    )(
        pick,
        count,
        pool_images[:, :, 0, :],
        pool_targets.reshape(POOL, columns * maps, batch),
        weights,
        master_slots[0, 0],
        accum_slots[0, 0],
    )
    matches = (owner_map[:, None] == numbers[None, :]).astype(jnp.int32)
    owner_of = jnp.sum(numbers[:, None] * matches, axis=0)
    working_next = jnp.take(fetched, owner_of ^ me, axis=0, mode="clip").reshape(weights.shape)[None]
    return (working_next, master_next[None, None], accum_next[None, None])


def solution(mesh):
    placed = (
        P("rep", "site", None, None, None),
        P("site", "rep", None, None, None),
        P("site", "rep", None, None, None),
        P(None, None, "site", None),
        P(None, "site", None, None, None),
        P(),
        P(),
    )
    return jax.shard_map(
        per_device,
        mesh=mesh,
        in_specs=placed,
        out_specs=(
            P("site", None, None, None),
            P("site", "rep", None, None, None),
            P("site", "rep", None, None, None),
        ),
        check_vma=False,
    )
```

time: 389 us -> 116 us (0.30)
  waiting for transfers between devices: 185 us -> 0 us
  Pallas kernels: 0 us -> 102 us
  matrix products: 74 us -> 0 us
  local copies, waits for them, and re-layouts: 51.8 us -> 10.2 us
  starting transfers between devices: 37.5 us -> 0 us
  between operations: 20.6 us -> 0.66 us
  other arithmetic: 17.8 us -> 2.71 us
    pallas_call x0 -> x1, Pallas kernels: none -> 102 us  [per_device(): pl.pallas_call(functools.partial(step_kernel, sites), out_shape=(jax.Shap...]
    ppermute x12 -> x0, waiting for transfers between devices: 78.1 us -> none  [passed_along(): return lax.ppermute(shard, axis, pairs)]
    dot_general x3 -> x0, matrix products: 74 us -> none  [per_device(): jnp.einsum('cob,bck->cok', signal, patches, preferred_element_type=jnp.fl...]
    reduce_scatter x1 -> x0, waiting for transfers between devices: 54.8 us -> none  [per_device(): lax.psum_scatter(ordered, 'rep', scatter_dimension=0, tiled=True)]
    all_gather x1 -> x0, waiting for transfers between devices: 51.8 us -> none  [per_device(): lax.all_gather(master_next[0].astype(jnp.bfloat16), 'rep', axis=0, tiled=...]
    ppermute x12 -> x0, starting transfers between devices: 37.4 us -> none  [passed_along(): return lax.ppermute(shard, axis, pairs)]
    transpose x3 -> x0, local copies, waits for them, and re-layouts: 20.4 us -> none  [build_patches(): stacked.transpose(0, 3, 1, 2, 4)]
    unnamed x84 -> x7, local copies, waits for them, and re-layouts: 15.9 us -> 4.69 us
  transfers between devices with their start and end apart: 14 -> 0, of which waited for: 9 -> 0; matrix products, arithmetic and copies ran while one was open for 20% -> 0% of each run, Pallas kernels for 0% -> 0%
where the time goes in v1:
time: 116 us
  Pallas kernels  102 us (88%)
  local copies, waits for them, and re-layouts  10.2 us (9%)
  other arithmetic  2.71 us (2%)
    pallas_call x1, Pallas kernels, per_device(): pl.pallas_call(functools.partial(step_kernel, sites), out_shape=(jax.Shap...  102 us
    gather x1, local copies, waits for them, and re-layouts, per_device(): jnp.take(fetched, owner_of ^ me, axis=0, mode='clip').reshape(weights.shape)  5.52 us
    unnamed x7, local copies, waits for them, and re-layouts  4.69 us

profile of v1, /device:TPU:17, one launch (start us, length us, event | category | flops | bytes accessed | tf_op | source)
XLA Modules:
  0.0 115.7 jit_solution(729543922561551633)
XLA Ops:
  0.6 0.7 select_reduce_fusion
  1.4 0.8 copy.10
  2.1 0.7 convert_reduce_fusion.count_ref
  2.8 1.3 %fusion.pick_ref = f32[4,4]{1,0:T(4,128)} fusion(s32[4]{0:T(128)} %param.13), kind=kLoop, calls=%fused_computation.6 | loop fusion | flops 32 | bytes 80 | tf_op jit(solution)/shard_map/convert_element_type | solution.py:587
  4.1 102.1 %step.1 = (bf16[4,4,64,2304]{3,2,1,0:T(8,128)(2,1)}, f32[4,64,2304]{2,1,0:T(8,128)}, f32[4,64,2304]{2,1,0:T(8,128)}) custom-call(f32[4,4]{1,0:T(4,128)} %fusion.pick_ref, f32[4,4]{1,0:T(4,128)} %convert_reduce_fusion.count_ref, bf16[4,256,1024]{2,1,0:T(8,128)(2,1)} %bitcast.14, bf16[4,1024,256]{2,1,0:T(8,128)(2,1)} %bitcast.15, ...), custom_call_target="tpu_custom_call" | custom-call | tf_op jit(solution)/shard_map/step/pallas_call | solution.py:592
  106.2 0.0 copy-start.1
  106.2 5.5 %gather_fusion = bf16[4,4,64,2304]{3,2,1,0:T(8,128)(2,1)} fusion(bf16[4,4,64,2304]{3,2,1,0:T(8,128)(2,1)} %get-tuple-element.6, s32[1024]{0:T(1024)S(1)} %pad_clamp_fusion), kind=kCustom, calls=%fused_computation | custom fusion | bytes 9437200 | tf_op jit(solution)/shard_map/jit(_take)/gather | solution.py:654
  111.8 0.0 copy-done.1
  111.8 0.0 copy-start
  111.8 1.4 %copy.13 = f32[1,1,4,64,2304]{4,3,2,1,0:T(8,128)} copy(f32[1,1,4,64,2304]{4,3,2,1,0:T(8,128)S(1)} %bitcast.11) | data formatting | bytes 4718592
  113.2 1.1 copy-done
  114.3 1.4 %copy.14 = f32[1,1,4,64,2304]{4,3,2,1,0:T(8,128)} copy(f32[1,1,4,64,2304]{4,3,2,1,0:T(8,128)S(1)} %bitcast.10) | data formatting | bytes 4718592
  (2 shorter events, 0.0 us)
Async XLA Ops:
  106.2 5.5 %copy-start.1 = (f32[4,64,2304]{2,1,0:T(8,128)S(1)}, f32[4,64,2304]{2,1,0:T(8,128)}, u32[]{:S(2)}) copy-start(f32[4,64,2304]{2,1,0:T(8,128)} %get-tuple-element.7) | copy-start | bytes 7077892
  111.8 2.5 %copy-start = (f32[4,64,2304]{2,1,0:T(8,128)S(1)}, f32[4,64,2304]{2,1,0:T(8,128)}, u32[]{:S(2)}) copy-start(f32[4,64,2304]{2,1,0:T(8,128)} %get-tuple-element.8) | copy-start | bytes 7077892

commit v2 on v1

--- a/solution.py
+++ b/solution.py
@@ -17,7 +17,7 @@
 TAPS = FIELD * CH
 BAND = 640
 LEFT = 128
-HALVES = 2
+PIECES = 4
 OWN = 2
 FACTOR = (FIELD * FIELD * CH) ** (-0.5)
 LEARNING_RATE = 0.3
@@ -28,8 +28,8 @@
 
 def step_kernel(
     sites,
-    pick_ref,
-    count_ref,
+    index_ref,
+    owner_ref,
     images_ref,
     targets_ref,
     working_ref,
@@ -83,8 +83,7 @@
     x = [x0, x1, x2, x3, x4, x5]
     batch = images_ref.shape[1]
     width = images_ref.shape[2]
-    piece = batch // HALVES
-    duo = 2 * piece
+    piece = batch // PIECES
     span = POOL * piece
 
     g = lax.axis_index("rep")
@@ -105,7 +104,31 @@
     has_ahead = s + 2 < sites
     has_behind = s >= 2
     valid = [(s + d - 2 >= 0) & (s + d - 2 < sites) for d in range(FIELD)]
-    halves = range(HALVES)
+
+    def same(a, b):
+        return (1 - jnp.minimum(jnp.abs(a - b), 1)).astype(jnp.float32)
+
+    pick = [[same(owner_ref[peer(k)], block) for block in range(REPS)] for k in range(REPS)]
+    entry = lax.broadcasted_iota(jnp.int32, (1, span), 1) // piece
+    count = []
+    for k in range(2):
+        of_lane = jnp.zeros((1, span), jnp.float32)
+        for p in range(POOL):
+            times = sum(same(index_ref[peer(k), m], p) for m in range(MICRO))
+            of_lane = jnp.where(entry == p, times, of_lane)
+        count.append(of_lane)
+
+    barrier = pltpu.get_barrier_semaphore()
+    for device in (across, partner, sibling):
+        pl.semaphore_signal(barrier, inc=1, device_id=device, device_id_type=MESH)
+
+    @pl.when(has_ahead)
+    def _():
+        pl.semaphore_signal(barrier, inc=1, device_id=ahead, device_id_type=MESH)
+
+    @pl.when(has_behind)
+    def _():
+        pl.semaphore_signal(barrier, inc=1, device_id=behind, device_id_type=MESH)
 
     def own_image(p, h):
         return pltpu.make_async_copy(
@@ -120,7 +143,7 @@
         pltpu.make_async_copy(master_ref, master, sem_load.at[POOL + 2, 0]),
         pltpu.make_async_copy(accum_ref, accum, sem_load.at[POOL + 3, 0]),
     ]
-    for h in halves:
+    for h in range(PIECES):
         for p in range(POOL):
             own_image(p, h).start()
     for load in loads:
@@ -135,18 +158,6 @@
             @pl.when(jnp.logical_not(valid[d]))
             def _(d=d):
                 x[d][:, LEFT : LEFT + width] = jnp.zeros((POOL * batch, width), jnp.bfloat16)
-
-    barrier = pltpu.get_barrier_semaphore()
-    for device in (across, partner, sibling):
-        pl.semaphore_signal(barrier, inc=1, device_id=device, device_id_type=MESH)
-
-    @pl.when(has_ahead)
-    def _():
-        pl.semaphore_signal(barrier, inc=1, device_id=ahead, device_id_type=MESH)
-
-    @pl.when(has_behind)
-    def _():
-        pl.semaphore_signal(barrier, inc=1, device_id=behind, device_id_type=MESH)
 
     pl.semaphore_wait(barrier, 3 + has_ahead.astype(jnp.int32) + has_behind.astype(jnp.int32))
 
@@ -177,32 +188,38 @@
             device_id_type=MESH,
         )
 
-    def natives(h):
-        for p in range(POOL):
-            own_image(p, h).wait()
+    def natives():
+        for h in range(PIECES):
+            for p in range(POOL):
+                own_image(p, h).wait()
 
         @pl.when(has_ahead)
         def _():
             for i in (0, 1):
-                link(OWN, 0, q[i], h, ahead, send_a.at[i, h]).start()
+                for h in range(PIECES):
+                    link(OWN, 0, q[i], h, ahead, send_a.at[i, h]).start()
 
         @pl.when(has_behind)
         def _():
             for i in (1, 0):
-                link(OWN, 4, q[i], h, behind, send_b.at[i, h]).start()
+                for h in range(PIECES):
+                    link(OWN, 4, q[i], h, behind, send_b.at[i, h]).start()
 
         @pl.when(even)
         def _():
-            link(OWN, 1, q[0], h, across, send_c.at[0, h]).start()
+            for h in range(PIECES):
+                link(OWN, 1, q[0], h, across, send_c.at[0, h]).start()
 
             @pl.when(s == 0)
             def _():
-                link(OWN, 1, q[1], h, across, send_c.at[1, h]).start()
+                for h in range(PIECES):
+                    link(OWN, 1, q[1], h, across, send_c.at[1, h]).start()
 
         @pl.when(odd == 1)
         def _():
             for i in (1, 0):
-                link(OWN, 3, q[i], h, across, send_c.at[i, h]).start()
+                for h in range(PIECES):
+                    link(OWN, 3, q[i], h, across, send_c.at[i, h]).start()
 
     def passed(slot, p, h, *sends):
         @pl.when(valid[slot])
@@ -263,6 +280,7 @@
         def _():
             passed(3, q[1], h)
 
+    def arrivals_four(h):
         passed(5, q[1], h)
         for slot in (0, 1, 3, 4, 5):
 
@@ -299,25 +317,21 @@
                 )
         return carry
 
-    def forward(h, n, low, high):
-        at = h * span + n * duo
+    def forward(h, low, high):
+        at = slice(h * span, (h + 1) * span)
 
         def one_block(block, carry):
             lanes = pl.multiple_of(block * (CB * CH), CB * CH)
-            total = jnp.zeros((CB * MAPS, duo), jnp.float32)
-            for d in range(FIELD):
-                total = total + lax.dot_general(
-                    banded[block, :, d * BAND : (d + 1) * BAND],
-                    x[d][at : at + duo, pl.ds(lanes, BAND)],
-                    (((1,), (1,)), ((), ())),
-                    preferred_element_type=jnp.float32,
-                )
+            patches = jnp.concatenate([x[d][at, pl.ds(lanes, BAND)] for d in range(FIELD)], axis=1)
+            total = lax.dot_general(
+                banded[block], patches, (((1,), (1,)), ((), ())), preferred_element_type=jnp.float32
+            )
             active = jnp.tanh(FACTOR * total)
             of_block = pl.ds(pl.multiple_of(block * (CB * MAPS), CB * MAPS), CB * MAPS)
-            of_half = slice(h * piece, (h + 1) * piece)
+            of_piece = slice(h * piece, (h + 1) * piece)
             wanted = jnp.concatenate(
-                [targets[2 * n, of_block, of_half], targets[2 * n + 1, of_block, of_half]], axis=1
-            ).astype(jnp.float32)
+                [targets[p, of_block, of_piece].astype(jnp.float32) for p in range(POOL)], axis=1
+            )
             signal[block] = ((active - wanted) * (1.0 - active * active)).astype(jnp.bfloat16)
             return carry
 
@@ -325,7 +339,7 @@
 
     strip = 32
 
-    def select(h, n):
+    def select(h):
         def one_strip(i, carry):
             at = pl.ds(pl.multiple_of(i * strip, strip), strip)
             parts = [signal[block, at, :] for block in range(REPS)]
@@ -333,71 +347,62 @@
             for k in range(REPS):
                 taken = None
                 for block in range(REPS):
-                    scale = jnp.full((strip, duo), pick_ref[peer(k), block], jnp.float32)
+                    scale = jnp.full((strip, span), pick[k][block], jnp.float32)
                     term = scale.astype(jnp.bfloat16) * parts[block]
                     taken = term if taken is None else taken + term
                 results.append(taken)
-            own[h, n, at, :] = results[0]
-            chosen[h, n, 0, at, :] = results[1]
-            kept[h, n, at, :] = results[2]
-            chosen[h, n, 1, at, :] = results[3]
+            own[h, at, :] = results[0]
+            chosen[h, 0, at, :] = results[1]
+            kept[h, at, :] = results[2]
+            chosen[h, 1, at, :] = results[3]
             return carry
 
         lax.fori_loop(0, CB * MAPS // strip, one_strip, 0)
-
-    def choice(h, n):
+        choice(h).start()
+
+    def choice(h):
         return pltpu.make_async_remote_copy(
-            src_ref=chosen.at[h, n],
-            dst_ref=chosen_in.at[h, n],
-            send_sem=send_s.at[h, n],
-            recv_sem=recv_s.at[h, n],
+            src_ref=chosen.at[h],
+            dst_ref=chosen_in.at[h],
+            send_sem=send_s.at[h],
+            recv_sem=recv_s.at[h],
             device_id=sibling,
             device_id_type=MESH,
         )
 
-    def pair_copy(h, n):
+    def pair_copy(h):
         return pltpu.make_async_remote_copy(
-            src_ref=pair.at[h, n],
-            dst_ref=pair_in.at[h, n],
-            send_sem=send_p.at[h, n],
-            recv_sem=recv_p.at[h, n],
+            src_ref=pair.at[h],
+            dst_ref=pair_in.at[h],
+            send_sem=send_p.at[h],
+            recv_sem=recv_p.at[h],
             device_id=partner,
             device_id_type=MESH,
         )
 
-    def weighed(k, n, value):
-        value = value.astype(jnp.float32)
-        return jnp.concatenate(
-            [
-                count_ref[peer(k), 2 * n] * value[:, :piece],
-                count_ref[peer(k), 2 * n + 1] * value[:, piece:],
-            ],
-            axis=1,
-        )
-
-    def make_pair(h, n):
-        choice(h, n).wait_recv()
+    def make_pair(h):
+        choice(h).wait_recv()
 
         def one_strip(i, carry):
             at = pl.ds(pl.multiple_of(i * strip, strip), strip)
-            pair[h, n, at, :] = (
-                weighed(0, n, kept[h, n, at, :]) + weighed(1, n, chosen_in[h, n, 1, at, :])
+            pair[h, at, :] = (
+                count[0] * kept[h, at, :].astype(jnp.float32)
+                + count[1] * chosen_in[h, 1, at, :].astype(jnp.float32)
             ).astype(jnp.bfloat16)
             return carry
 
         lax.fori_loop(0, CB * MAPS // strip, one_strip, 0)
-        pair_copy(h, n).start()
-
-    def combine(h, n):
-        pair_copy(h, n).wait_recv()
-        lanes = slice(h * span + n * duo, h * span + (n + 1) * duo)
+        pair_copy(h).start()
+
+    def combine(h):
+        pair_copy(h).wait_recv()
 
         def one_strip(i, carry):
             at = pl.ds(pl.multiple_of(i * strip, strip), strip)
-            combined[at, lanes] = (
-                weighed(0, n, own[h, n, at, :])
-                + weighed(1, n, chosen_in[h, n, 0, at, :])
-                + pair_in[h, n, at, :].astype(jnp.float32)
+            combined[at, h * span : (h + 1) * span] = (
+                count[0] * own[h, at, :].astype(jnp.float32)
+                + count[1] * chosen_in[h, 0, at, :].astype(jnp.float32)
+                + pair_in[h, at, :].astype(jnp.float32)
             ).astype(jnp.bfloat16)
             return carry
 
@@ -409,7 +414,7 @@
             for d in range(FIELD):
                 taken = None
                 for block in range(REPS):
-                    scale = jnp.full((strip, BAND), pick_ref[g, block], jnp.float32)
+                    scale = jnp.full((strip, BAND), pick[0][block], jnp.float32)
                     lanes = slice(block * CB * CH, block * CB * CH + BAND)
                     term = scale.astype(jnp.bfloat16) * x[d][at, lanes]
                     taken = term if taken is None else taken + term
@@ -418,41 +423,29 @@
 
         lax.fori_loop(0, span // strip, one_strip, 0)
 
-    natives(0)
+    natives()
     loads[0].wait()
     lax.fori_loop(0, REPS, band_weights, 0)
     for load in loads[1:]:
         load.wait()
-    arrivals_one(0)
-    arrivals_two(0)
-    natives(1)
+    for h in range(PIECES):
+        arrivals_one(h)
+    for h in range(PIECES):
+        arrivals_two(h)
     arrivals_three(0)
-    forward(0, 0, 0, REPS)
-    select(0, 0)
-    choice(0, 0).start()
-    arrivals_one(1)
-    forward(0, 1, 0, REPS)
-    make_pair(0, 0)
-    select(0, 1)
-    choice(0, 1).start()
-    arrivals_two(1)
-    make_pair(0, 1)
-    own_window(0)
-    combine(0, 0)
-    combine(0, 1)
-    arrivals_three(1)
-    forward(1, 0, 0, REPS)
-    select(1, 0)
-    choice(1, 0).start()
-    forward(1, 1, 0, REPS // 2)
-    make_pair(1, 0)
-    forward(1, 1, REPS // 2, REPS)
-    select(1, 1)
-    choice(1, 1).start()
-    own_window(1)
-    make_pair(1, 1)
-    combine(1, 0)
-    combine(1, 1)
+    for h in range(PIECES):
+        if h + 1 < PIECES:
+            arrivals_three(h + 1)
+        arrivals_four(h)
+        forward(h, 0, REPS // 2)
+        if h:
+            make_pair(h - 1)
+        forward(h, REPS // 2, REPS)
+        select(h)
+        own_window(h)
+    make_pair(PIECES - 1)
+    for h in range(PIECES):
+        combine(h)
 
     def part_of(ref, d):
         return ref.at[:, :, pl.ds(d * TAPS, TAPS)]
@@ -548,10 +541,10 @@
             store.wait()
         store_theirs(d).wait()
         pass_beside(d).wait()
-    for h in halves:
-        for n in range(POOL // 2):
-            choice(h, n).wait_send()
-            pair_copy(h, n).wait_send()
+    pieces = range(PIECES)
+    for h in pieces:
+        choice(h).wait_send()
+        pair_copy(h).wait_send()
 
     def all_sent(condition, sems):
         @pl.when(condition)
@@ -559,17 +552,63 @@
             for sem in sems:
                 link(OWN, OWN, 0, 0, partner, sem).wait_send()
 
-    all_sent(has_ahead, [send_a.at[i, h] for i in (0, 1) for h in halves])
-    all_sent(has_behind, [send_b.at[i, h] for i in (0, 1) for h in halves])
-    all_sent(s >= 0, [send_c.at[0, h] for h in halves])
-    all_sent((odd == 1) | (s == 0), [send_c.at[1, h] for h in halves])
-    all_sent((even & has_ahead) | ((odd == 1) & has_behind), [send_d.at[0, h] for h in halves])
-    all_sent(even & has_ahead, [send_d.at[1, h] for h in halves])
-    all_sent(has_ahead, [send_e.at[h] for h in halves])
-    all_sent(has_behind & valid[3], [send_f.at[h] for h in halves])
-    all_sent(valid[5], [send_g.at[h] for h in halves])
+    all_sent(has_ahead, [send_a.at[i, h] for i in (0, 1) for h in pieces])
+    all_sent(has_behind, [send_b.at[i, h] for i in (0, 1) for h in pieces])
+    all_sent(s >= 0, [send_c.at[0, h] for h in pieces])
+    all_sent((odd == 1) | (s == 0), [send_c.at[1, h] for h in pieces])
+    all_sent((even & has_ahead) | ((odd == 1) & has_behind), [send_d.at[0, h] for h in pieces])
+    all_sent(even & has_ahead, [send_d.at[1, h] for h in pieces])
+    all_sent(has_ahead, [send_e.at[h] for h in pieces])
+    all_sent(has_behind & valid[3], [send_f.at[h] for h in pieces])
+    all_sent(valid[5], [send_g.at[h] for h in pieces])
     for slot in (0, 1, 3, 4, 5):
-        all_sent(valid[slot], [send_x.at[slot, j, h] for j in (0, 1) for h in halves])
+        all_sent(valid[slot], [send_x.at[slot, j, h] for j in (0, 1) for h in pieces])
+
+
+def place_kernel(
+    pieces,
+    owner_ref,
+    fetched_ref,
+    master_ref,
+    accum_ref,
+    working_out,
+    master_out,
+    accum_out,
+    fetched,
+    master,
+    accum,
+    sem_in,
+    sem_out,
+):
+    g = lax.axis_index("rep")
+    columns = CB // pieces
+    moves = []
+    for block in range(REPS):
+        owner = 0
+        for i in range(REPS):
+            owner = jnp.where(owner_ref[i] == block, i, owner)
+        k = 2 * ((owner // 2 + g // 2) % 2) + (owner + g) % 2
+        for piece in range(pieces):
+            at = pl.ds(block * CB + piece * columns, columns)
+            moves.append(
+                (
+                    fetched_ref.at[k, pl.ds(piece * columns, columns)],
+                    fetched.at[at],
+                    working_out.at[at],
+                )
+            )
+    for cc in range(CB):
+        moves.append((master_ref.at[cc], master.at[cc], master_out.at[cc]))
+        moves.append((accum_ref.at[cc], accum.at[cc], accum_out.at[cc]))
+    into = [pltpu.make_async_copy(a, b, sem_in.at[i]) for i, (a, b, _) in enumerate(moves)]
+    out = [pltpu.make_async_copy(b, c, sem_out.at[i]) for i, (_, b, c) in enumerate(moves)]
+    for copy in into:
+        copy.start()
+    for first, second in zip(into, out):
+        first.wait()
+        second.start()
+    for copy in out:
+        copy.wait()
 
 
 def per_device(
@@ -581,11 +620,7 @@
     weights = working[0, 0]
     columns, maps, kdim = weights.shape
     padded = width - CB * CH + BAND
-    duo = 2 * (batch // HALVES)
-    me = lax.axis_index("rep")
-    numbers = jnp.arange(REPS, dtype=jnp.int32)
-    pick = (owner_map[:, None] == numbers).astype(jnp.float32)
-    count = jnp.sum((batch_index[:, :, None] == numbers).astype(jnp.float32), axis=1)
+    span = POOL * (batch // PIECES)
     any_space = pl.BlockSpec(memory_space=pl.ANY)
     smem = pl.BlockSpec(memory_space=pltpu.SMEM)
     dma = pltpu.SemaphoreType.DMA
@@ -603,13 +638,13 @@
             pltpu.VMEM((columns, maps, kdim), jnp.bfloat16),
             pltpu.VMEM((REPS, CB * maps, FIELD * BAND), jnp.bfloat16),
             pltpu.VMEM((POOL, columns * maps, batch), jnp.bfloat16),
-            pltpu.VMEM((REPS, CB * maps, duo), jnp.bfloat16),
-            pltpu.VMEM((HALVES, 2, 2, CB * maps, duo), jnp.bfloat16),
-            pltpu.VMEM((HALVES, 2, 2, CB * maps, duo), jnp.bfloat16),
-            pltpu.VMEM((HALVES, 2, CB * maps, duo), jnp.bfloat16),
-            pltpu.VMEM((HALVES, 2, CB * maps, duo), jnp.bfloat16),
-            pltpu.VMEM((HALVES, 2, CB * maps, duo), jnp.bfloat16),
-            pltpu.VMEM((HALVES, 2, CB * maps, duo), jnp.bfloat16),
+            pltpu.VMEM((REPS, CB * maps, span), jnp.bfloat16),
+            pltpu.VMEM((PIECES, 2, CB * maps, span), jnp.bfloat16),
+            pltpu.VMEM((PIECES, 2, CB * maps, span), jnp.bfloat16),
+            pltpu.VMEM((PIECES, CB * maps, span), jnp.bfloat16),
+            pltpu.VMEM((PIECES, CB * maps, span), jnp.bfloat16),
+            pltpu.VMEM((PIECES, CB * maps, span), jnp.bfloat16),
+            pltpu.VMEM((PIECES, CB * maps, span), jnp.bfloat16),
             pltpu.VMEM((CB * maps, POOL * batch), jnp.bfloat16),
             pltpu.VMEM((FIELD, POOL * batch, BAND), jnp.bfloat16),
             pltpu.VMEM((CB, maps, kdim), jnp.float32),
@@ -617,21 +652,21 @@
             pltpu.VMEM((CB, maps, kdim), jnp.bfloat16),
             pltpu.VMEM((CB, maps, kdim), jnp.bfloat16),
             pltpu.VMEM((CB * maps, BAND), jnp.float32),
-            dma((POOL + 4, HALVES)),
-            dma((2, HALVES)),
-            dma((2, HALVES)),
-            dma((2, HALVES)),
-            dma((2, HALVES)),
-            dma((HALVES,)),
-            dma((HALVES,)),
-            dma((HALVES,)),
-            dma((FIELD, 2, HALVES)),
-            dma((FIELD, 2, HALVES)),
-            dma((FIELD, 2, HALVES)),
-            dma((HALVES, 2)),
-            dma((HALVES, 2)),
-            dma((HALVES, 2)),
-            dma((HALVES, 2)),
+            dma((POOL + 4, PIECES)),
+            dma((2, PIECES)),
+            dma((2, PIECES)),
+            dma((2, PIECES)),
+            dma((2, PIECES)),
+            dma((PIECES,)),
+            dma((PIECES,)),
+            dma((PIECES,)),
+            dma((FIELD, 2, PIECES)),
+            dma((FIELD, 2, PIECES)),
+            dma((FIELD, 2, PIECES)),
+            dma((PIECES,)),
+            dma((PIECES,)),
+            dma((PIECES,)),
+            dma((PIECES,)),
             dma((3, FIELD)),
             dma((3, FIELD)),
             dma((4, FIELD)),
@@ -641,17 +676,35 @@
         ),
         name="step",
     )(
-        pick,
-        count,
+        batch_index,
+        owner_map,
         pool_images[:, :, 0, :],
         pool_targets.reshape(POOL, columns * maps, batch),
         weights,
         master_slots[0, 0],
         accum_slots[0, 0],
     )
-    matches = (owner_map[:, None] == numbers[None, :]).astype(jnp.int32)
-    owner_of = jnp.sum(numbers[:, None] * matches, axis=0)
-    working_next = jnp.take(fetched, owner_of ^ me, axis=0, mode="clip").reshape(weights.shape)[None]
+    pieces = 2
+    working_next, master_next, accum_next = pl.pallas_call(
+        functools.partial(place_kernel, pieces),
+        out_shape=(
+            jax.ShapeDtypeStruct((columns, maps, kdim), jnp.bfloat16),
+            jax.ShapeDtypeStruct((CB, maps, kdim), jnp.float32),
+            jax.ShapeDtypeStruct((CB, maps, kdim), jnp.float32),
+        ),
+        in_specs=[smem] + [any_space] * 3,
+        out_specs=(any_space, any_space, any_space),
+        scratch_shapes=[
+            pltpu.VMEM((columns, maps, kdim), jnp.bfloat16),
+            pltpu.VMEM((CB, maps, kdim), jnp.float32),
+            pltpu.VMEM((CB, maps, kdim), jnp.float32),
+            dma((REPS * pieces + 2 * CB,)),
+            dma((REPS * pieces + 2 * CB,)),
+        ],
+        compiler_params=pltpu.CompilerParams(vmem_limit_bytes=62 * 1024 * 1024),
+        name="place",
+    )(owner_map, fetched, master_next, accum_next)
+    working_next = working_next[None]
     return (working_next, master_next[None, None], accum_next[None, None])
 
 

time: 116 us -> 113 us (0.974)
  local copies, waits for them, and re-layouts: 10.2 us -> 0 us
  Pallas kernels: 102 us -> 112 us
  other arithmetic: 2.71 us -> 0 us
    pallas_call x0 -> x1, Pallas kernels: none -> 8.14 us  [per_device(): pl.pallas_call(functools.partial(place_kernel, pieces), out_shape=(jax.Sh...]
    gather x1 -> x0, local copies, waits for them, and re-layouts: 5.52 us -> none  [per_device(): jnp.take(fetched, owner_of ^ me, axis=0, mode='clip').reshape(weights.shape)]
    unnamed x7 -> x0, local copies, waits for them, and re-layouts: 4.69 us -> none
    pallas_call x1, Pallas kernels: 102 us -> 104 us  [per_device(): pl.pallas_call(functools.partial(step_kernel, sites), out_shape=(jax.Shap...]
    reduce_sum x2 -> x0, other arithmetic: 1.4 us -> none  [the longest x1 0.74 us: per_device(): owner_of = jnp.sum(numbers[:, None] * matches, axis=0)]
    convert_element_type x1 -> x0, other arithmetic: 1.3 us -> none  [per_device(): pick = (owner_map[:, None] == numbers).astype(jnp.float32)]
where the time goes in v2:
time: 113 us
  Pallas kernels  112 us (99%)
    pallas_call x1, Pallas kernels, per_device(): pl.pallas_call(functools.partial(step_kernel, sites), out_shape=(jax.Shap...  104 us
    pallas_call x1, Pallas kernels, per_device(): pl.pallas_call(functools.partial(place_kernel, pieces), out_shape=(jax.Sh...  8.14 us

profile of v2, /device:TPU:17, one launch (start us, length us, event | category | flops | bytes accessed | tf_op | source)
XLA Modules:
  0.0 112.8 jit_solution(8635213908941791640)
XLA Ops:
  0.6 104.1 %step.1 = (bf16[4,4,64,2304]{3,2,1,0:T(8,128)(2,1)}, f32[4,64,2304]{2,1,0:T(8,128)}, f32[4,64,2304]{2,1,0:T(8,128)}) custom-call(s32[4,3]{1,0:T(4,128)} %index_ref.1, s32[4]{0:T(128)} %owner_ref.3, bf16[4,256,1024]{2,1,0:T(8,128)(2,1)} %bitcast.11, bf16[4,1024,256]{2,1,0:T(8,128)(2,1)} %bitcast.12, bf16[16,64,2304]{2,1,0:T(8,128)(2,1)} %bitcast.8, ...), custom_call_target="tpu_custom_call" | custom-call | tf_op jit(solution)/shard_map/step/pallas_call | solution.py:627
  104.7 8.1 %place.1 = (bf16[16,64,2304]{2,1,0:T(8,128)(2,1)}, f32[4,64,2304]{2,1,0:T(8,128)}, f32[4,64,2304]{2,1,0:T(8,128)}) custom-call(s32[4]{0:T(128)} %owner_ref.3, bf16[4,4,64,2304]{3,2,1,0:T(8,128)(2,1)} %get-tuple-element.9.fetched_ref, f32[4,64,2304]{2,1,0:T(8,128)} %get-tuple-element.10.master_ref, f32[4,64,2304]{2,1,0:T(8,128)} %get-tuple-element.11.accum_ref), custom_call_target="tpu_custom_call" | custom-call | tf_op jit(solution)/shard_map/place/pallas_call | solution.py:688

commit v3 on v2

--- a/solution.py
+++ b/solution.py
@@ -18,6 +18,8 @@
 BAND = 640
 LEFT = 128
 PIECES = 4
+EARLY = (0, 2, 4)
+LATE = (1, 3, 5)
 OWN = 2
 FACTOR = (FIELD * FIELD * CH) ** (-0.5)
 LEARNING_RATE = 0.3
@@ -56,10 +58,7 @@
     pair_in,
     combined,
     window,
-    master,
-    accum,
-    mine,
-    theirs,
+    partial,
     grad,
     sem_load,
     send_a,
@@ -78,7 +77,6 @@
     recv_p,
     send_w,
     recv_w,
-    sem_store,
 ):
     x = [x0, x1, x2, x3, x4, x5]
     batch = images_ref.shape[1]
@@ -140,8 +138,8 @@
     loads = [
         pltpu.make_async_copy(working_ref, weights, sem_load.at[POOL, 0]),
         pltpu.make_async_copy(targets_ref, targets, sem_load.at[POOL + 1, 0]),
-        pltpu.make_async_copy(master_ref, master, sem_load.at[POOL + 2, 0]),
-        pltpu.make_async_copy(accum_ref, accum, sem_load.at[POOL + 3, 0]),
+        pltpu.make_async_copy(master_ref, master_out, sem_load.at[POOL + 2, 0]),
+        pltpu.make_async_copy(accum_ref, accum_out, sem_load.at[POOL + 3, 0]),
     ]
     for h in range(PIECES):
         for p in range(POOL):
@@ -210,11 +208,6 @@
             for h in range(PIECES):
                 link(OWN, 1, q[0], h, across, send_c.at[0, h]).start()
 
-            @pl.when(s == 0)
-            def _():
-                for h in range(PIECES):
-                    link(OWN, 1, q[1], h, across, send_c.at[1, h]).start()
-
         @pl.when(odd == 1)
         def _():
             for i in (1, 0):
@@ -253,7 +246,7 @@
         def _():
             passed(0, q[0], h, (has_behind, link(0, 1, q[0], h, across, send_d.at[0, h])))
             passed(4, q[1], h)
-            passed(1, q[1], h)
+            passed(1, q[1], h, (s == 1, link(1, 1, q[1], h, partner, send_b.at[1, h])))
 
     def arrivals_two(h):
         @pl.when(even)
@@ -282,7 +275,9 @@
 
     def arrivals_four(h):
         passed(5, q[1], h)
-        for slot in (0, 1, 3, 4, 5):
+
+    def handed(h, slots):
+        for slot in slots:
 
             @pl.when(valid[slot])
             def _(slot=slot):
@@ -298,7 +293,7 @@
 
     def band_weights(block, carry):
         for cc in range(CB):
-            for d in range(FIELD):
+            for place, d in enumerate(EARLY + LATE):
                 taps = weights[block * CB + cc, :, d * TAPS : (d + 1) * TAPS]
                 if cc % 2:
                     wide = jnp.concatenate(
@@ -312,20 +307,34 @@
                     parts = [jnp.zeros((MAPS, before), jnp.bfloat16)] + parts
                 if after:
                     parts = parts + [jnp.zeros((MAPS, after), jnp.bfloat16)]
-                banded[block, cc * MAPS : (cc + 1) * MAPS, d * BAND : (d + 1) * BAND] = (
+                banded[block, cc * MAPS : (cc + 1) * MAPS, place * BAND : (place + 1) * BAND] = (
                     jnp.concatenate(parts, axis=1)
                 )
         return carry
 
+    half_taps = len(EARLY) * BAND
+
+    def product(h, block, slots, taps):
+        at = slice(h * span, (h + 1) * span)
+        lanes = pl.multiple_of(block * (CB * CH), CB * CH)
+        patches = jnp.concatenate([x[d][at, pl.ds(lanes, BAND)] for d in slots], axis=1)
+        return lax.dot_general(
+            banded[block, :, taps],
+            patches,
+            (((1,), (1,)), ((), ())),
+            preferred_element_type=jnp.float32,
+        )
+
+    def early(h):
+        def one_block(block, carry):
+            partial[h, block] = product(h, block, EARLY, slice(0, half_taps))
+            return carry
+
+        lax.fori_loop(0, REPS, one_block, 0)
+
     def forward(h, low, high):
-        at = slice(h * span, (h + 1) * span)
-
         def one_block(block, carry):
-            lanes = pl.multiple_of(block * (CB * CH), CB * CH)
-            patches = jnp.concatenate([x[d][at, pl.ds(lanes, BAND)] for d in range(FIELD)], axis=1)
-            total = lax.dot_general(
-                banded[block], patches, (((1,), (1,)), ((), ())), preferred_element_type=jnp.float32
-            )
+            total = partial[h, block] + product(h, block, LATE, slice(half_taps, 2 * half_taps))
             active = jnp.tanh(FACTOR * total)
             of_block = pl.ds(pl.multiple_of(block * (CB * MAPS), CB * MAPS), CB * MAPS)
             of_piece = slice(h * piece, (h + 1) * piece)
@@ -408,10 +417,10 @@
 
         lax.fori_loop(0, CB * MAPS // strip, one_strip, 0)
 
-    def own_window(h):
+    def own_window(h, slots):
         def one_strip(i, carry):
             at = pl.ds(pl.multiple_of(h * span + i * strip, strip), strip)
-            for d in range(FIELD):
+            for d in slots:
                 taken = None
                 for block in range(REPS):
                     scale = jnp.full((strip, BAND), pick[0][block], jnp.float32)
@@ -432,17 +441,20 @@
         arrivals_one(h)
     for h in range(PIECES):
         arrivals_two(h)
-    arrivals_three(0)
     for h in range(PIECES):
-        if h + 1 < PIECES:
-            arrivals_three(h + 1)
+        handed(h, (0, 4))
+        early(h)
+        own_window(h, EARLY)
+        arrivals_three(h)
+    for h in range(PIECES):
         arrivals_four(h)
+        handed(h, LATE)
         forward(h, 0, REPS // 2)
         if h:
             make_pair(h - 1)
         forward(h, REPS // 2, REPS)
         select(h)
-        own_window(h)
+        own_window(h, LATE)
     make_pair(PIECES - 1)
     for h in range(PIECES):
         combine(h)
@@ -450,55 +462,28 @@
     def part_of(ref, d):
         return ref.at[:, :, pl.ds(d * TAPS, TAPS)]
 
+    def block_copy(source, target, d, device, sems):
+        return pltpu.make_async_remote_copy(
+            src_ref=part_of(fetched_ref.at[source], d),
+            dst_ref=part_of(fetched_ref.at[target], d),
+            send_sem=send_w.at[sems, d],
+            recv_sem=recv_w.at[sems, d],
+            device_id=device,
+            device_id_type=MESH,
+        )
+
     def send_across(d):
-        return pltpu.make_async_remote_copy(
-            src_ref=part_of(mine, d),
-            dst_ref=part_of(theirs, d),
-            send_sem=send_w.at[0, d],
-            recv_sem=recv_w.at[0, d],
-            device_id=partner,
-            device_id_type=MESH,
-        )
+        return block_copy(0, 2, d, partner, 0)
 
     def send_beside(d):
-        return pltpu.make_async_remote_copy(
-            src_ref=part_of(mine, d),
-            dst_ref=part_of(fetched_ref.at[1], d),
-            send_sem=send_w.at[1, d],
-            recv_sem=recv_w.at[1, d],
-            device_id=sibling,
-            device_id_type=MESH,
-        )
+        return block_copy(0, 1, d, sibling, 1)
 
     def pass_beside(d):
-        return pltpu.make_async_remote_copy(
-            src_ref=part_of(theirs, d),
-            dst_ref=part_of(fetched_ref.at[3], d),
-            send_sem=send_w.at[2, d],
-            recv_sem=recv_w.at[2, d],
-            device_id=sibling,
-            device_id_type=MESH,
-        )
-
-    def stores(d):
-        return [
-            pltpu.make_async_copy(
-                part_of(mine, d), part_of(fetched_ref.at[0], d), sem_store.at[0, d]
-            ),
-            pltpu.make_async_copy(part_of(master, d), part_of(master_out, d), sem_store.at[1, d]),
-            pltpu.make_async_copy(part_of(accum, d), part_of(accum_out, d), sem_store.at[2, d]),
-        ]
-
-    def store_theirs(d):
-        return pltpu.make_async_copy(
-            part_of(theirs, d), part_of(fetched_ref.at[2], d), sem_store.at[3, d]
-        )
+        return block_copy(2, 3, d, sibling, 2)
 
     def send_part(d):
         send_across(d).start()
         send_beside(d).start()
-        for store in stores(d):
-            store.start()
 
     for d in range(FIELD):
         for at in range(0, BAND, 256):
@@ -520,26 +505,22 @@
                 column = grad[of_column, before : before + TAPS]
             slot_grad = FACTOR * column
             taps = slice(d * TAPS, (d + 1) * TAPS)
-            accum_next = accum[cc, :, taps] + slot_grad * slot_grad
-            master_next = master[cc, :, taps] - LEARNING_RATE * slot_grad / (
+            accum_next = accum_out[cc, :, taps] + slot_grad * slot_grad
+            master_next = master_out[cc, :, taps] - LEARNING_RATE * slot_grad / (
                 jnp.sqrt(accum_next) + EPSILON
             )
-            accum[cc, :, taps] = accum_next
-            master[cc, :, taps] = master_next
-            mine[cc, :, taps] = master_next.astype(jnp.bfloat16)
+            accum_out[cc, :, taps] = accum_next
+            master_out[cc, :, taps] = master_next
+            fetched_ref[0, cc, :, taps] = master_next.astype(jnp.bfloat16)
 
     send_part(FIELD - 1)
     for d in range(FIELD):
         send_across(d).wait_recv()
         pass_beside(d).start()
-        store_theirs(d).start()
 
     for d in range(FIELD):
         send_across(d).wait_send()
         send_beside(d).wait()
-        for store in stores(d):
-            store.wait()
-        store_theirs(d).wait()
         pass_beside(d).wait()
     pieces = range(PIECES)
     for h in pieces:
@@ -555,7 +536,8 @@
     all_sent(has_ahead, [send_a.at[i, h] for i in (0, 1) for h in pieces])
     all_sent(has_behind, [send_b.at[i, h] for i in (0, 1) for h in pieces])
     all_sent(s >= 0, [send_c.at[0, h] for h in pieces])
-    all_sent((odd == 1) | (s == 0), [send_c.at[1, h] for h in pieces])
+    all_sent(odd == 1, [send_c.at[1, h] for h in pieces])
+    all_sent(s == 1, [send_b.at[1, h] for h in pieces])
     all_sent((even & has_ahead) | ((odd == 1) & has_behind), [send_d.at[0, h] for h in pieces])
     all_sent(even & has_ahead, [send_d.at[1, h] for h in pieces])
     all_sent(has_ahead, [send_e.at[h] for h in pieces])
@@ -566,48 +548,26 @@
 
 
 def place_kernel(
-    pieces,
-    owner_ref,
-    fetched_ref,
-    master_ref,
-    accum_ref,
-    working_out,
-    master_out,
-    accum_out,
-    fetched,
-    master,
-    accum,
-    sem_in,
-    sem_out,
+    owner_ref, fetched, master, accum, working_out, master_out, accum_out, sem_out
 ):
     g = lax.axis_index("rep")
-    columns = CB // pieces
     moves = []
     for block in range(REPS):
         owner = 0
         for i in range(REPS):
             owner = jnp.where(owner_ref[i] == block, i, owner)
         k = 2 * ((owner // 2 + g // 2) % 2) + (owner + g) % 2
-        for piece in range(pieces):
-            at = pl.ds(block * CB + piece * columns, columns)
+        for cc in range(0, CB, 2):
             moves.append(
-                (
-                    fetched_ref.at[k, pl.ds(piece * columns, columns)],
-                    fetched.at[at],
-                    working_out.at[at],
-                )
+                (fetched.at[k, pl.ds(cc, 2)], working_out.at[pl.ds(block * CB + cc, 2)])
             )
     for cc in range(CB):
-        moves.append((master_ref.at[cc], master.at[cc], master_out.at[cc]))
-        moves.append((accum_ref.at[cc], accum.at[cc], accum_out.at[cc]))
-    into = [pltpu.make_async_copy(a, b, sem_in.at[i]) for i, (a, b, _) in enumerate(moves)]
-    out = [pltpu.make_async_copy(b, c, sem_out.at[i]) for i, (_, b, c) in enumerate(moves)]
-    for copy in into:
+        moves.append((master.at[cc], master_out.at[cc]))
+        moves.append((accum.at[cc], accum_out.at[cc]))
+    copies = [pltpu.make_async_copy(a, b, sem_out.at[i]) for i, (a, b) in enumerate(moves)]
+    for copy in copies:
         copy.start()
-    for first, second in zip(into, out):
-        first.wait()
-        second.start()
-    for copy in out:
+    for copy in copies:
         copy.wait()
 
 
@@ -623,16 +583,17 @@
     span = POOL * (batch // PIECES)
     any_space = pl.BlockSpec(memory_space=pl.ANY)
     smem = pl.BlockSpec(memory_space=pltpu.SMEM)
+    vmem = pl.BlockSpec(memory_space=pltpu.VMEM)
     dma = pltpu.SemaphoreType.DMA
     fetched, master_next, accum_next = pl.pallas_call(
         functools.partial(step_kernel, sites),
         out_shape=(
-            jax.ShapeDtypeStruct((REPS, CB, maps, kdim), jnp.bfloat16),
-            jax.ShapeDtypeStruct((CB, maps, kdim), jnp.float32),
-            jax.ShapeDtypeStruct((CB, maps, kdim), jnp.float32),
+            pltpu.VMEM((REPS, CB, maps, kdim), jnp.bfloat16),
+            pltpu.VMEM((CB, maps, kdim), jnp.float32),
+            pltpu.VMEM((CB, maps, kdim), jnp.float32),
         ),
         in_specs=[smem, smem] + [any_space] * 5,
-        out_specs=(any_space, any_space, any_space),
+        out_specs=(vmem, vmem, vmem),
         scratch_shapes=[pltpu.VMEM((POOL * batch, padded), jnp.bfloat16)] * FIELD
         + [
             pltpu.VMEM((columns, maps, kdim), jnp.bfloat16),
@@ -647,10 +608,7 @@
             pltpu.VMEM((PIECES, CB * maps, span), jnp.bfloat16),
             pltpu.VMEM((CB * maps, POOL * batch), jnp.bfloat16),
             pltpu.VMEM((FIELD, POOL * batch, BAND), jnp.bfloat16),
-            pltpu.VMEM((CB, maps, kdim), jnp.float32),
-            pltpu.VMEM((CB, maps, kdim), jnp.float32),
-            pltpu.VMEM((CB, maps, kdim), jnp.bfloat16),
-            pltpu.VMEM((CB, maps, kdim), jnp.bfloat16),
+            pltpu.VMEM((PIECES, REPS, CB * maps, span), jnp.float32),
             pltpu.VMEM((CB * maps, BAND), jnp.float32),
             dma((POOL + 4, PIECES)),
             dma((2, PIECES)),
@@ -669,10 +627,9 @@
             dma((PIECES,)),
             dma((3, FIELD)),
             dma((3, FIELD)),
-            dma((4, FIELD)),
         ],
         compiler_params=pltpu.CompilerParams(
-            collective_id=0, has_side_effects=True, vmem_limit_bytes=62 * 1024 * 1024
+            collective_id=0, has_side_effects=True, vmem_limit_bytes=52 * 1024 * 1024
         ),
         name="step",
     )(
@@ -684,24 +641,17 @@
         master_slots[0, 0],
         accum_slots[0, 0],
     )
-    pieces = 2
     working_next, master_next, accum_next = pl.pallas_call(
-        functools.partial(place_kernel, pieces),
+        place_kernel,
         out_shape=(
             jax.ShapeDtypeStruct((columns, maps, kdim), jnp.bfloat16),
             jax.ShapeDtypeStruct((CB, maps, kdim), jnp.float32),
             jax.ShapeDtypeStruct((CB, maps, kdim), jnp.float32),
         ),
-        in_specs=[smem] + [any_space] * 3,
+        in_specs=[smem, vmem, vmem, vmem],
         out_specs=(any_space, any_space, any_space),
-        scratch_shapes=[
-            pltpu.VMEM((columns, maps, kdim), jnp.bfloat16),
-            pltpu.VMEM((CB, maps, kdim), jnp.float32),
-            pltpu.VMEM((CB, maps, kdim), jnp.float32),
-            dma((REPS * pieces + 2 * CB,)),
-            dma((REPS * pieces + 2 * CB,)),
-        ],
-        compiler_params=pltpu.CompilerParams(vmem_limit_bytes=62 * 1024 * 1024),
+        scratch_shapes=[dma((4 * CB,))],
+        compiler_params=pltpu.CompilerParams(vmem_limit_bytes=16 * 1024 * 1024),
         name="place",
     )(owner_map, fetched, master_next, accum_next)
     working_next = working_next[None]

time: 113 us -> 99.3 us (0.88)
  the two profiles are of different devices: /device:TPU:17 before, /device:TPU:97 now
where the time goes in v3:
time: 99.3 us; the launch traced here: 99.2 us
  Pallas kernels  98.5 us (99%)
    pallas_call x1, Pallas kernels, per_device(): pl.pallas_call(functools.partial(step_kernel, sites), out_shape=(pltpu.VM...  94.2 us
    pallas_call x1, Pallas kernels, per_device(): pl.pallas_call(place_kernel, out_shape=(jax.ShapeDtypeStruct((columns, ma...  4.32 us

profile of v3, /device:TPU:97, one launch (start us, length us, event | category | flops | bytes accessed | tf_op | source)
XLA Modules:
  0.0 99.2 jit_solution(12157511710734783389)
XLA Ops:
  0.6 0.0 copy-start
  0.6 94.2 %step.1 = (bf16[4,4,64,2304]{3,2,1,0:T(8,128)(2,1)S(1)}, f32[4,64,2304]{2,1,0:T(8,128)S(1)}, f32[4,64,2304]{2,1,0:T(8,128)S(1)}) custom-call(s32[4,3]{1,0:T(4,128)} %index_ref.1, s32[4]{0:T(128)} %owner_ref.3, bf16[4,256,1024]{2,1,0:T(8,128)(2,1)} %bitcast.11, bf16[4,1024,256]{2,1,0:T(8,128)(2,1)} %bitcast.12, bf16[16,64,2304]{2,1,0:T(8,128)(2,1)} %bitcast.8, ...), custom_call_target="tpu_custom_call" | custom-call | tf_op jit(solution)/shard_map/step/pallas_call | solution.py:588
  94.8 0.0 copy-done
  94.8 4.3 %place.1 = (bf16[16,64,2304]{2,1,0:T(8,128)(2,1)}, f32[4,64,2304]{2,1,0:T(8,128)}, f32[4,64,2304]{2,1,0:T(8,128)}) custom-call(s32[4]{0:T(128)S(1)} %copy-done, bf16[4,4,64,2304]{3,2,1,0:T(8,128)(2,1)S(1)} %get-tuple-element.9.fetched, f32[4,64,2304]{2,1,0:T(8,128)S(1)} %get-tuple-element.10.master, f32[4,64,2304]{2,1,0:T(8,128)S(1)} %get-tuple-element.11.accum), custom_call_target="tpu_custom_call" | custom-call | tf_op jit(solution)/shard_map/place/pallas_call | solution.py:644
Async XLA Ops:
  0.6 94.2 %copy-start = (s32[4]{0:T(128)S(1)}, s32[4]{0:T(128)}, u32[]{:S(2)}) copy-start(s32[4]{0:T(128)} %owner_ref.3) | copy-start | bytes 52

commit v4 on v3

--- a/solution.py
+++ b/solution.py
@@ -59,6 +59,7 @@
     combined,
     window,
     partial,
+    wanted,
     grad,
     sem_load,
     send_a,
@@ -186,33 +187,27 @@
             device_id_type=MESH,
         )
 
-    def natives():
-        for h in range(PIECES):
-            for p in range(POOL):
-                own_image(p, h).wait()
+    def natives(h):
+        for p in range(POOL):
+            own_image(p, h).wait()
 
         @pl.when(has_ahead)
         def _():
             for i in (0, 1):
-                for h in range(PIECES):
-                    link(OWN, 0, q[i], h, ahead, send_a.at[i, h]).start()
+                link(OWN, 0, q[i], h, ahead, send_a.at[i, h]).start()
 
         @pl.when(has_behind)
         def _():
+            link(OWN, 4, q[1], h, behind, send_b.at[1, h]).start()
+
+        @pl.when(even)
+        def _():
+            link(OWN, 1, q[0], h, across, send_c.at[0, h]).start()
+
+        @pl.when(odd == 1)
+        def _():
             for i in (1, 0):
-                for h in range(PIECES):
-                    link(OWN, 4, q[i], h, behind, send_b.at[i, h]).start()
-
-        @pl.when(even)
-        def _():
-            for h in range(PIECES):
-                link(OWN, 1, q[0], h, across, send_c.at[0, h]).start()
-
-        @pl.when(odd == 1)
-        def _():
-            for i in (1, 0):
-                for h in range(PIECES):
-                    link(OWN, 3, q[i], h, across, send_c.at[i, h]).start()
+                link(OWN, 3, q[i], h, across, send_c.at[i, h]).start()
 
     def passed(slot, p, h, *sends):
         @pl.when(valid[slot])
@@ -226,55 +221,61 @@
 
             hand_over(slot, p, h).start()
 
-    def onward(h):
-        return (
-            (has_ahead, link(3, 1, q[0], h, ahead, send_e.at[h])),
-            (has_behind, link(3, 5, q[0], h, behind, send_f.at[h])),
-        )
-
-    def swap(h):
-        return (valid[5], link(5, 5, q[0], h, partner, send_g.at[h]))
-
-    def arrivals_one(h):
+    def onward(i, h):
+        behind_copy = (has_behind, link(3, 5, q[i], h, behind, send_f.at[i, h]))
+        if i:
+            return (behind_copy,)
+        return (has_ahead, link(3, 1, q[0], h, ahead, send_e.at[h])), behind_copy
+
+    def below_first(h):
+        swap = (s >= 0, link(4, 4, q[1], h, partner, send_g.at[h]))
+
         @pl.when(even)
         def _():
-            passed(4, q[1], h, (has_ahead, link(4, 3, q[1], h, across, send_d.at[1, h])))
-            passed(3, q[0], h, *onward(h))
+            passed(4, q[1], h, swap, (has_ahead, link(4, 3, q[1], h, across, send_d.at[1, h])))
+
+        @pl.when(odd == 1)
+        def _():
+            passed(4, q[1], h, swap)
+            passed(1, q[1], h, (s == 1, link(1, 1, q[1], h, partner, send_b.at[0, h])))
+
+    def below_second(h):
+        @pl.when(even)
+        def _():
+            passed(4, q[0], h, (has_ahead, link(4, 3, q[0], h, across, send_d.at[0, h])))
+
+        @pl.when(odd == 1)
+        def _():
+            passed(4, q[0], h)
+
+    def straight(h):
+        @pl.when(even)
+        def _():
+            passed(3, q[0], h, *onward(0, h))
             passed(0, q[0], h)
+            passed(3, q[1], h, *onward(1, h))
 
         @pl.when(odd == 1)
         def _():
             passed(0, q[0], h, (has_behind, link(0, 1, q[0], h, across, send_d.at[0, h])))
-            passed(4, q[1], h)
-            passed(1, q[1], h, (s == 1, link(1, 1, q[1], h, partner, send_b.at[1, h])))
-
-    def arrivals_two(h):
+
+        passed(0, q[1], h)
+
+    def crossed(i, h):
+        @pl.when(odd == 1)
+        def _():
+            passed(3, q[i], h, *onward(i, h))
+
+    def last_rows(h):
+        passed(5, q[0], h)
+        passed(1, q[0], h)
+
         @pl.when(even)
         def _():
-            passed(4, q[0], h, (has_ahead, link(4, 3, q[0], h, across, send_d.at[0, h])))
-            passed(3, q[1], h)
-            passed(0, q[1], h)
-
-        @pl.when(odd == 1)
-        def _():
-            passed(3, q[0], h, *onward(h))
-            passed(4, q[0], h)
-            passed(0, q[1], h)
-
-    def arrivals_three(h):
-        passed(5, q[0], h, swap(h))
-        passed(1, q[0], h)
-
-        @pl.when(even)
-        def _():
             passed(1, q[1], h)
 
-        @pl.when(odd == 1)
-        def _():
-            passed(3, q[1], h)
-
-    def arrivals_four(h):
         passed(5, q[1], h)
+        handed(h, LATE)
 
     def handed(h, slots):
         for slot in slots:
@@ -326,22 +327,27 @@
         )
 
     def early(h):
+        handed(h, (0, 4))
+
         def one_block(block, carry):
             partial[h, block] = product(h, block, EARLY, slice(0, half_taps))
+            of_block = pl.ds(pl.multiple_of(block * (CB * MAPS), CB * MAPS), CB * MAPS)
+            of_piece = slice(h * piece, (h + 1) * piece)
+            wanted[h, of_block, :] = jnp.concatenate(
+                [targets[p, of_block, of_piece].astype(jnp.float32) for p in range(POOL)], axis=1
+            ).astype(jnp.bfloat16)
             return carry
 
         lax.fori_loop(0, REPS, one_block, 0)
+        own_window(h, EARLY)
 
     def forward(h, low, high):
         def one_block(block, carry):
             total = partial[h, block] + product(h, block, LATE, slice(half_taps, 2 * half_taps))
             active = jnp.tanh(FACTOR * total)
             of_block = pl.ds(pl.multiple_of(block * (CB * MAPS), CB * MAPS), CB * MAPS)
-            of_piece = slice(h * piece, (h + 1) * piece)
-            wanted = jnp.concatenate(
-                [targets[p, of_block, of_piece].astype(jnp.float32) for p in range(POOL)], axis=1
-            )
-            signal[block] = ((active - wanted) * (1.0 - active * active)).astype(jnp.bfloat16)
+            gap = active - wanted[h, of_block, :].astype(jnp.float32)
+            signal[block] = (gap * (1.0 - active * active)).astype(jnp.bfloat16)
             return carry
 
         lax.fori_loop(low, high, one_block, 0)
@@ -432,29 +438,49 @@
 
         lax.fori_loop(0, span // strip, one_strip, 0)
 
-    natives()
-    loads[0].wait()
-    lax.fori_loop(0, REPS, band_weights, 0)
-    for load in loads[1:]:
-        load.wait()
-    for h in range(PIECES):
-        arrivals_one(h)
-    for h in range(PIECES):
-        arrivals_two(h)
-    for h in range(PIECES):
-        handed(h, (0, 4))
-        early(h)
-        own_window(h, EARLY)
-        arrivals_three(h)
-    for h in range(PIECES):
-        arrivals_four(h)
-        handed(h, LATE)
+    def finish(h):
+        last_rows(h)
         forward(h, 0, REPS // 2)
         if h:
             make_pair(h - 1)
         forward(h, REPS // 2, REPS)
         select(h)
         own_window(h, LATE)
+
+    for h in range(PIECES):
+        natives(h)
+    loads[0].wait()
+    lax.fori_loop(0, REPS, band_weights, 0)
+    for load in loads[1:]:
+        load.wait()
+    below_first(0)
+    below_first(1)
+    straight(0)
+    below_second(0)
+    below_first(2)
+    below_second(1)
+    below_first(3)
+    straight(1)
+    below_second(2)
+    below_second(3)
+    early(0)
+    crossed(0, 0)
+    crossed(0, 1)
+    straight(2)
+    early(1)
+    crossed(1, 0)
+    crossed(0, 2)
+    straight(3)
+    early(2)
+    crossed(1, 1)
+    early(3)
+    crossed(0, 3)
+    finish(0)
+    crossed(1, 2)
+    finish(1)
+    crossed(1, 3)
+    finish(2)
+    finish(3)
     make_pair(PIECES - 1)
     for h in range(PIECES):
         combine(h)
@@ -534,15 +560,15 @@
                 link(OWN, OWN, 0, 0, partner, sem).wait_send()
 
     all_sent(has_ahead, [send_a.at[i, h] for i in (0, 1) for h in pieces])
-    all_sent(has_behind, [send_b.at[i, h] for i in (0, 1) for h in pieces])
+    all_sent(has_behind, [send_b.at[1, h] for h in pieces])
     all_sent(s >= 0, [send_c.at[0, h] for h in pieces])
     all_sent(odd == 1, [send_c.at[1, h] for h in pieces])
-    all_sent(s == 1, [send_b.at[1, h] for h in pieces])
+    all_sent(s == 1, [send_b.at[0, h] for h in pieces])
     all_sent((even & has_ahead) | ((odd == 1) & has_behind), [send_d.at[0, h] for h in pieces])
     all_sent(even & has_ahead, [send_d.at[1, h] for h in pieces])
     all_sent(has_ahead, [send_e.at[h] for h in pieces])
-    all_sent(has_behind & valid[3], [send_f.at[h] for h in pieces])
-    all_sent(valid[5], [send_g.at[h] for h in pieces])
+    all_sent(has_behind & valid[3], [send_f.at[i, h] for i in (0, 1) for h in pieces])
+    all_sent(valid[4], [send_g.at[h] for h in pieces])
     for slot in (0, 1, 3, 4, 5):
         all_sent(valid[slot], [send_x.at[slot, j, h] for j in (0, 1) for h in pieces])
 
@@ -609,6 +635,7 @@
             pltpu.VMEM((CB * maps, POOL * batch), jnp.bfloat16),
             pltpu.VMEM((FIELD, POOL * batch, BAND), jnp.bfloat16),
             pltpu.VMEM((PIECES, REPS, CB * maps, span), jnp.float32),
+            pltpu.VMEM((PIECES, columns * maps, span), jnp.bfloat16),
             pltpu.VMEM((CB * maps, BAND), jnp.float32),
             dma((POOL + 4, PIECES)),
             dma((2, PIECES)),
@@ -616,7 +643,7 @@
             dma((2, PIECES)),
             dma((2, PIECES)),
             dma((PIECES,)),
-            dma((PIECES,)),
+            dma((2, PIECES)),
             dma((PIECES,)),
             dma((FIELD, 2, PIECES)),
             dma((FIELD, 2, PIECES)),

time: 99.3 us -> 97.8 us (0.985)
  the two profiles are of different devices: /device:TPU:97 before, /device:TPU:17 now
where the time goes in v4:
time: 97.8 us; the launch traced here: 97.7 us
  Pallas kernels  97 us (99%)
    pallas_call x1, Pallas kernels, per_device(): pl.pallas_call(functools.partial(step_kernel, sites), out_shape=(pltpu.VM...  92.7 us
    pallas_call x1, Pallas kernels, per_device(): pl.pallas_call(place_kernel, out_shape=(jax.ShapeDtypeStruct((columns, ma...  4.32 us

profile of v4, /device:TPU:17, one launch (start us, length us, event | category | flops | bytes accessed | tf_op | source)
XLA Modules:
  0.0 97.7 jit_solution(12295711496386991047)
XLA Ops:
  0.6 0.0 copy-start
  0.6 92.7 %step.1 = (bf16[4,4,64,2304]{3,2,1,0:T(8,128)(2,1)S(1)}, f32[4,64,2304]{2,1,0:T(8,128)S(1)}, f32[4,64,2304]{2,1,0:T(8,128)S(1)}) custom-call(s32[4,3]{1,0:T(4,128)} %index_ref.1, s32[4]{0:T(128)} %owner_ref.3, bf16[4,256,1024]{2,1,0:T(8,128)(2,1)} %bitcast.11, bf16[4,1024,256]{2,1,0:T(8,128)(2,1)} %bitcast.12, bf16[16,64,2304]{2,1,0:T(8,128)(2,1)} %bitcast.8, ...), custom_call_target="tpu_custom_call" | custom-call | tf_op jit(solution)/shard_map/step/pallas_call | solution.py:614
  93.4 0.0 copy-done
  93.4 4.3 %place.1 = (bf16[16,64,2304]{2,1,0:T(8,128)(2,1)}, f32[4,64,2304]{2,1,0:T(8,128)}, f32[4,64,2304]{2,1,0:T(8,128)}) custom-call(s32[4]{0:T(128)S(1)} %copy-done, bf16[4,4,64,2304]{3,2,1,0:T(8,128)(2,1)S(1)} %get-tuple-element.9.fetched, f32[4,64,2304]{2,1,0:T(8,128)S(1)} %get-tuple-element.10.master, f32[4,64,2304]{2,1,0:T(8,128)S(1)} %get-tuple-element.11.accum), custom_call_target="tpu_custom_call" | custom-call | tf_op jit(solution)/shard_map/place/pallas_call | solution.py:671
Async XLA Ops:
  0.6 92.7 %copy-start = (s32[4]{0:T(128)S(1)}, s32[4]{0:T(128)}, u32[]{:S(2)}) copy-start(s32[4]{0:T(128)} %owner_ref.3) | copy-start | bytes 52

commit v5 on v4

--- a/solution.py
+++ b/solution.py
@@ -237,6 +237,10 @@
         @pl.when(odd == 1)
         def _():
             passed(4, q[1], h, swap)
+
+    def above(h):
+        @pl.when(odd == 1)
+        def _():
             passed(1, q[1], h, (s == 1, link(1, 1, q[1], h, partner, send_b.at[0, h])))
 
     def below_second(h):
@@ -463,6 +467,8 @@
     straight(1)
     below_second(2)
     below_second(3)
+    for h in range(PIECES):
+        above(h)
     early(0)
     crossed(0, 0)
     crossed(0, 1)

time: 97.8 us -> 95.9 us (0.981)
  Pallas kernels: 97 us -> 94.3 us
    pallas_call x1, Pallas kernels: 92.7 us -> 90 us  [per_device(): pl.pallas_call(functools.partial(step_kernel, sites), out_shape=(pltpu.VM...]
where the time goes in v5:
time: 95.9 us; the launch traced here: 94.9 us
  Pallas kernels  94.3 us (98%)
    pallas_call x1, Pallas kernels, per_device(): pl.pallas_call(functools.partial(step_kernel, sites), out_shape=(pltpu.VM...  90 us
    pallas_call x1, Pallas kernels, per_device(): pl.pallas_call(place_kernel, out_shape=(jax.ShapeDtypeStruct((columns, ma...  4.32 us

profile of v5, /device:TPU:17, one launch (start us, length us, event | category | flops | bytes accessed | tf_op | source)
XLA Modules:
  0.0 94.9 jit_solution(14047288251667012981)
XLA Ops:
  0.6 0.0 copy-start
  0.6 90.0 %step.1 = (bf16[4,4,64,2304]{3,2,1,0:T(8,128)(2,1)S(1)}, f32[4,64,2304]{2,1,0:T(8,128)S(1)}, f32[4,64,2304]{2,1,0:T(8,128)S(1)}) custom-call(s32[4,3]{1,0:T(4,128)} %index_ref.1, s32[4]{0:T(128)} %owner_ref.3, bf16[4,256,1024]{2,1,0:T(8,128)(2,1)} %bitcast.11, bf16[4,1024,256]{2,1,0:T(8,128)(2,1)} %bitcast.12, bf16[16,64,2304]{2,1,0:T(8,128)(2,1)} %bitcast.8, ...), custom_call_target="tpu_custom_call" | custom-call | tf_op jit(solution)/shard_map/step/pallas_call | solution.py:620
  90.6 0.0 copy-done
  90.6 4.3 %place.1 = (bf16[16,64,2304]{2,1,0:T(8,128)(2,1)}, f32[4,64,2304]{2,1,0:T(8,128)}, f32[4,64,2304]{2,1,0:T(8,128)}) custom-call(s32[4]{0:T(128)S(1)} %copy-done, bf16[4,4,64,2304]{3,2,1,0:T(8,128)(2,1)S(1)} %get-tuple-element.9.fetched, f32[4,64,2304]{2,1,0:T(8,128)S(1)} %get-tuple-element.10.master, f32[4,64,2304]{2,1,0:T(8,128)S(1)} %get-tuple-element.11.accum), custom_call_target="tpu_custom_call" | custom-call | tf_op jit(solution)/shard_map/place/pallas_call | solution.py:677
Async XLA Ops:
  0.6 90.0 %copy-start = (s32[4]{0:T(128)S(1)}, s32[4]{0:T(128)}, u32[]{:S(2)}) copy-start(s32[4]{0:T(128)} %owner_ref.3) | copy-start | bytes 52
